TPU v7x, 512 devices: a whole 4x8x8 slice. The times are simulated.
512 devices in a mesh: grp: 4 (over z_hi, core), lrn: 128 (over x, z_lo, y).
Axes of the slice: x: 4, y: 8, z: 8 (z_hi: 2, z_lo: 4; z = z_hi * 4 + z_lo), core: 2. Of those that a mesh axis runs over, the one named last changes fastest.
Arguments:
- aerosol_mass: float32 [4, 32, 65536], P(None, None, ('grp', 'lrn')), may hold values from 0.001 to 0.1
- size_bins: int32 [4, 32, 65536], P(None, None, ('grp', 'lrn')), may hold values from 0 to 63
- cloud_tau: float32 [32, 65536], P(None, ('grp', 'lrn')), may hold values from 0.02 to 2
- cloud_mask: int32 [65536], P(('grp', 'lrn')), may hold values 0 or 1
- absorber: float32 [32, 65536], P(None, ('grp', 'lrn')), may hold values from 0.3 to 3
- surface_albedo: float32 [14, 65536], P(None, ('grp', 'lrn')), may hold values from 0.05 to 0.85
- cos_zenith: float32 [65536], P(('grp', 'lrn')), may hold values from 0.15 to 1
- ext_table: float32 [112, 256], replicated, may hold values from 0.2 to 2
- ssa_table: float32 [112, 256], replicated, may hold values from 0.5 to 0.95
- asym_table: float32 [112, 256], replicated, may hold values from 0.3 to 0.8
- gas_coeff: float32 [112], replicated, may hold values from 0.001 to 0.5
- solar_flux: float32 [112], replicated, may hold values from 0.3 to 3
- band_map: int32 [112], replicated, may hold values from 0 to 13
- column_learner: int32 [65536, 1], P(('grp', 'lrn')), may hold values from 0 to 127; in each aligned block of 128 rows (0 to 127, 128 to 255, ...) at most 2 rows name the same one
- trunk_weight: bfloat16 [2048, 256], P('lrn'), may hold values from -0.375 to 0.375
- trunk_bias: bfloat16 [2048], P('lrn'), may hold values from -3 to 3
- head_weight: bfloat16 [128, 2048, 128], P('lrn'), may hold values from -0.125 to 0.125
Outputs:
- fluxes: float32 [128, 65536], P(None, ('grp', 'lrn'))
- head_grad: float32 [128, 2048, 128], P('lrn')
- trunk_grad: float32 [2048, 256], P('lrn')
- bias_grad: float32 [2048], P('lrn')
Inputs may be any that keep to these rules, and one draw needn't show every extreme that they name: `column_learner`: in each aligned block of 128 rows (the columns of one device) no learner is named more than 2 times, a bound that some block reaches.
All inputs are finite; a program needn't handle non-finite values. No bound on the sum of `cloud_mask` on one device may be relied on, other than what follows from the above.
Results may differ from a plain program's by a relative error of at most 0.0019.
Values may be sent and summed in bfloat16 or wider, within the bound.
A program may use at most 64 MiB of HBM per device.

v0:
```python
from functools import partial
import math

import jax
import jax.numpy as jnp
from jax import lax
from jax.sharding import Mesh
from jax.sharding import PartitionSpec as P

COL_DEV = 128
LRN = ("lrn_0", "lrn_1", "lrn_2")
GRP_LRN = ("grp", "lrn_0", "lrn_1", "lrn_2")


CLOUD_SSA = 0.99
CLOUD_ASYM = 0.85
PRECISE = lax.Precision.HIGHEST


def in_one_piece(arrays, axis, split_dim, concat_dim, along):
    columns = [a.reshape(*a.shape[:along], -1) for a in arrays]
    both = jnp.concatenate(columns, axis=along)
    whole, at, gathered = (
        lax.all_to_all(both, axis, split_axis=split_dim, concat_axis=concat_dim, tiled=True),
        0,
        [],
    )
    for a, column in zip(arrays, columns):
        piece = whole[..., at : at + column.shape[along]]
        gathered.append(piece.reshape(*piece.shape[:along], *a.shape[along:]))
        at += column.shape[along]
    return tuple(gathered)


def from_everyone(x, axis):
    devices = lax.axis_size(axis)
    return lax.all_to_all(jnp.broadcast_to(x[None], (devices, *x.shape)), axis, 0, 0, tiled=True)


def joined_along(pieces, dim):
    lengths = list(pieces.shape[1:])
    lengths[dim] *= pieces.shape[0]
    return jnp.moveaxis(pieces, 0, dim).reshape(lengths)


def gathered_by_axis(x, axes, dim):
    far, near = axes
    pieces = from_everyone(from_everyone(x, far), near)
    return joined_along(pieces.swapaxes(0, 1).reshape(-1, *x.shape), dim)


def in_one_piece_2(arrays, axis, dim, along):
    columns = [a.reshape(*a.shape[:along], -1) for a in arrays]
    both = jnp.concatenate(columns, axis=along)
    whole, at, gathered = (gathered_by_axis(both, axis, dim), 0, [])
    for a, column in zip(arrays, columns):
        piece = whole[..., at : at + column.shape[along]]
        gathered.append(piece.reshape(*piece.shape[:along], *a.shape[along:]))
        at += column.shape[along]
    return tuple(gathered)


def in_blocks(x, dim, devices):
    lengths = x.shape
    pieces = x.reshape(*lengths[:dim], devices, lengths[dim] // devices, *lengths[dim + 1 :])
    return jnp.moveaxis(pieces, dim, 0)


def sent_and_summed(x, axis, dim):
    devices = lax.axis_size(axis)
    pieces = lax.all_to_all(in_blocks(x, dim, devices), axis, 0, 0, tiled=True)
    return jnp.sum(pieces, axis=0)


def collect(x, axis, dim):
    return joined_along(from_everyone(x, axis), dim)


def sent_and_summed_2(x, axis, dim):
    pieces = in_blocks(x, dim, lax.axis_size(axis))
    arrived = lax.all_to_all(pieces, axis, split_axis=0, concat_axis=0, tiled=True)
    return arrived.astype(jnp.float32).sum(axis=0)


def summed_rows(x, axes, dim):
    far, near = axes
    pieces = in_blocks(x, dim, lax.axis_size(far))
    nearer = sent_and_summed_2(pieces, near, dim + 1)
    arrived = lax.all_to_all(
        nearer.astype(jnp.bfloat16), far, split_axis=0, concat_axis=0, tiled=True
    )
    return arrived.astype(jnp.float32).sum(axis=0)


def in_one_piece_3(arrays, axis, dim, along):
    widths = [math.prod(a.shape[along:]) for a in arrays]
    both = jnp.concatenate(
        [a.reshape(*a.shape[:along], w) for a, w in zip(arrays, widths)], axis=along
    )
    whole = summed_rows(both, axis, dim)
    pieces = jnp.split(whole, [sum(widths[:k]) for k in range(1, len(widths))], axis=along)
    return tuple(
        (b.reshape(*whole.shape[:along], *a.shape[along:]) for a, b in zip(arrays, pieces))
    )


def taken_together(x, axis):
    return from_everyone(x, axis).sum(axis=0)


def packed_total(arrays, axis):
    ravelled, at, gathered = (jnp.concatenate([a.reshape(-1) for a in arrays]), 0, [])
    total = taken_together(ravelled, axis)
    for a in arrays:
        gathered.append(total[at : at + a.size].reshape(a.shape))
        at += a.size
    return tuple(gathered)


def optics_table(ext_table, ssa_table, asym_table):
    scatter = ext_table * ssa_table
    return jnp.concatenate([ext_table, scatter, scatter * asym_table], axis=0).astype(jnp.bfloat16)


def column_block(
    optic_table,
    gas_coeff,
    solar_flux,
    band_map,
    aerosol_mass,
    size_bins,
    cloud_tau,
    cloud_mask,
    absorber,
    surface_albedo,
    cos_zenith,
):
    mode_count, levels, width_cols = aerosol_mass.shape
    point_count = gas_coeff.shape[0]
    bin_count = optic_table.shape[1] // mode_count
    band_count = surface_albedo.shape[0]
    labels = jnp.arange(bin_count, dtype=jnp.int32)
    load_bf = aerosol_mass.astype(jnp.bfloat16)
    weights = jnp.where(
        size_bins[:, None] == labels[None, :, None, None],
        load_bf[:, None],
        jnp.zeros((), jnp.bfloat16),
    )
    weights = weights.reshape(mode_count * bin_count, levels * width_cols)
    optics = jnp.dot(optic_table, weights, preferred_element_type=jnp.float32).reshape(
        3, point_count, levels, width_cols
    )
    cloudy = (cloud_tau * cloud_mask.astype(jnp.float32)[None, :])[None]
    optical_depth = optics[0] + cloudy + gas_coeff[:, None, None] * absorber[None]
    scatter = optics[1] + CLOUD_SSA * cloudy
    forward = optics[2] + CLOUD_SSA * CLOUD_ASYM * cloudy
    single_albedo = scatter / optical_depth
    asym_factor = forward / scatter
    gamma_one = 2.0 - single_albedo * (1.0 + asym_factor)
    gamma_two = single_albedo * (1.0 - asym_factor)
    decay_rate = jnp.sqrt((gamma_one - gamma_two) * (gamma_one + gamma_two))
    damped = jnp.exp(-decay_rate * optical_depth)
    square = damped * damped
    denominator = decay_rate + gamma_one + (decay_rate - gamma_one) * square
    reflect = jnp.moveaxis(gamma_two * (1.0 - square) / denominator, 1, 0)
    transmit = jnp.moveaxis(2.0 * decay_rate * damped / denominator, 1, 0)
    band_hot = (band_map[:, None] == jnp.arange(band_count, dtype=jnp.int32)[None, :]).astype(
        jnp.float32
    )
    surface = jnp.dot(band_hot, surface_albedo, precision=PRECISE)
    source = solar_flux[:, None] * cos_zenith[None, :]

    def upward(below_reflect, layer):
        layer_reflect, layer_transmit = layer
        above = layer_reflect + layer_transmit * layer_transmit * below_reflect / (
            1.0 - layer_reflect * below_reflect
        )
        return (above, below_reflect)

    top_reflect, below_all = lax.scan(upward, surface, (reflect, transmit), reverse=True)

    def downward(down_now, layer):
        layer_reflect, layer_transmit, below_reflect = layer
        down_next = layer_transmit * down_now / (1.0 - layer_reflect * below_reflect)
        return (down_next, (down_next, below_reflect * down_next))

    _, (down_all, up_all) = lax.scan(downward, source, (reflect, transmit, below_all))
    upper = jnp.concatenate([(top_reflect * source)[None], up_all[:-1]], axis=0)
    group_hot = jnp.stack([band_map < band_count // 2, band_map >= band_count // 2]).astype(
        jnp.float32
    ) * (2.0 / point_count)
    down_flux = jnp.einsum("kg,lgc->klc", group_hot, down_all, precision=PRECISE)
    up_flux = jnp.einsum("kg,lgc->klc", group_hot, upper, precision=PRECISE)
    return jnp.stack([down_flux, up_flux], axis=1).reshape(4 * levels, width_cols)


def evolve(
    optic_table,
    gas_coeff,
    solar_flux,
    band_map,
    aerosol_mass,
    size_bins,
    cloud_tau,
    cloud_mask,
    absorber,
    surface_albedo,
    cos_zenith,
):
    total_cols = aerosol_mass.shape[-1]
    block_size = min(total_cols, 256)
    block_count = total_cols // block_size

    def splitter(array_in):
        return jnp.moveaxis(
            array_in.reshape(array_in.shape[:-1] + (block_count, block_size)), -2, 0
        )

    pieces = tuple(
        (
            splitter(array_in)
            for array_in in (
                aerosol_mass,
                size_bins,
                cloud_tau,
                cloud_mask,
                absorber,
                surface_albedo,
                cos_zenith,
            )
        )
    )

    def column_job(piece):
        return column_block(
            optic_table,
            gas_coeff,
            solar_flux,
            band_map,
            piece[0],
            piece[1],
            piece[2],
            piece[3],
            piece[4],
            piece[5],
            piece[6],
        )

    results = lax.map(column_job, pieces)
    return jnp.moveaxis(results, 0, 1).reshape(results.shape[1], total_cols)


def column_features(aerosol_mass, size_bins, bin_count):
    mode_count, levels, total_cols = aerosol_mass.shape
    first = (jnp.log(aerosol_mass) + 4.6) / 1.4
    second = (size_bins.astype(jnp.float32) - bin_count / 2) / (bin_count / 2)
    stacked = jnp.concatenate(
        [
            first.reshape(mode_count * levels, total_cols),
            second.reshape(mode_count * levels, total_cols),
        ],
        axis=0,
    )
    return stacked.astype(jnp.bfloat16)


def learner_terms(slot_rows, slot_goals, slot_valid, w_full, b_full, w_head, loss_scale):
    pre_act = (
        jnp.dot(slot_rows, w_full.T, preferred_element_type=jnp.float32)
        + b_full.astype(jnp.float32)[None, :]
    )
    active, slope = jax.vjp(partial(jax.nn.gelu, approximate=True), pre_act)
    hidden = active.astype(jnp.bfloat16)
    predicted = jnp.dot(hidden, w_head, preferred_element_type=jnp.float32)
    error_rows = (predicted - slot_goals.astype(jnp.float32)) * slot_valid.astype(jnp.float32)[
        :, None
    ]
    pred_grad = (error_rows * loss_scale).astype(jnp.bfloat16)
    hidden_grad = jnp.dot(pred_grad, w_head.T, preferred_element_type=jnp.float32)
    pre_grad = slope(hidden_grad)[0].astype(jnp.bfloat16)
    trunk_part = jnp.dot(pre_grad.T, slot_rows, preferred_element_type=jnp.float32)
    bias_part = jnp.sum(pre_grad, axis=0, dtype=jnp.float32)
    return (hidden, pred_grad, trunk_part, bias_part)


def per_device(
    aerosol_mass,
    size_bins,
    cloud_tau,
    cloud_mask,
    absorber,
    surface_albedo,
    cos_zenith,
    ext_table,
    ssa_table,
    asym_table,
    gas_coeff,
    solar_flux,
    band_map,
    column_learner,
    trunk_weight,
    trunk_bias,
    head_weight,
):
    optic_table = optics_table(ext_table, ssa_table, asym_table)
    fluxes = evolve(
        optic_table,
        gas_coeff,
        solar_flux,
        band_map,
        aerosol_mass,
        size_bins,
        cloud_tau,
        cloud_mask,
        absorber,
        surface_albedo,
        cos_zenith,
    )
    features = column_features(
        aerosol_mass, size_bins, optic_table.shape[1] // aerosol_mass.shape[0]
    )
    targets = fluxes.astype(jnp.bfloat16)
    columns_here = aerosol_mass.shape[-1]
    learners = lax.axis_size(LRN)
    capacity = 2 * columns_here // learners
    slot_count = learners * capacity
    destination = column_learner[:, 0]
    dest_hot = (destination[:, None] == jnp.arange(learners, dtype=jnp.int32)[None, :]).astype(
        jnp.int32
    )
    slot_rank = jnp.sum((jnp.cumsum(dest_hot, axis=0) - dest_hot) * dest_hot, axis=1)
    slot_index = destination * capacity + slot_rank
    dispatch = (jnp.arange(slot_count, dtype=jnp.int32)[:, None] == slot_index[None, :]).astype(
        jnp.bfloat16
    )
    packed = jnp.concatenate([features, targets], axis=0)
    slot_data = jnp.dot(dispatch, packed.T, preferred_element_type=jnp.float32).astype(jnp.bfloat16)
    feature_width = features.shape[0]
    row_feat = slot_data[:, :feature_width]
    row_goal = slot_data[:, feature_width:]
    filled = jnp.sum(dispatch, axis=1, dtype=jnp.float32).astype(jnp.bfloat16)
    slot_rows, slot_goals, slot_valid = in_one_piece((row_feat, row_goal, filled), LRN, 0, 0, 1)
    w_full, b_full = in_one_piece_2((trunk_weight, trunk_bias), ("lrn_0", ("lrn_1", "lrn_2")), 0, 1)
    hidden, pred_grad, trunk_part, bias_part = learner_terms(
        slot_rows, slot_goals, slot_valid, w_full, b_full, head_weight[0], 1.0 / COL_DEV
    )
    head_local = jnp.dot(hidden.T, pred_grad, preferred_element_type=jnp.float32)
    head_part = sent_and_summed(head_local, "grp", 0)
    head_sum = collect(head_part, "grp", 0)
    share_w, share_b = in_one_piece_3(
        (trunk_part.astype(jnp.bfloat16), bias_part.astype(jnp.bfloat16)),
        ("lrn_0", ("lrn_1", "lrn_2")),
        0,
        1,
    )
    trunk_grad, bias_grad = packed_total((share_w, share_b), "grp")
    return (fluxes, head_sum[None], trunk_grad, bias_grad)


def solution(mesh):
    split = Mesh(
        mesh.devices.reshape(mesh.shape["grp"], 4, 4, 8), ("grp", "lrn_0", "lrn_1", "lrn_2")
    )
    placed = (
        P(None, None, GRP_LRN),
        P(None, None, GRP_LRN),
        P(None, GRP_LRN),
        P(GRP_LRN),
        P(None, GRP_LRN),
        P(None, GRP_LRN),
        P(GRP_LRN),
        P(),
        P(),
        P(),
        P(),
        P(),
        P(),
        P(GRP_LRN, None),
        P(LRN, None),
        P(LRN),
        P(LRN, None, None),
    )
    return jax.shard_map(
        per_device,
        mesh=split,
        in_specs=placed,
        out_specs=(P(None, GRP_LRN), P(LRN, None, None), P(LRN, None), P(LRN)),
        check_vma=False,
    )
```

profile of v0, /device:TPU:64, one launch (start us, length us, event | category | flops | bytes accessed | tf_op | source)
XLA Modules:
  0.0 346.7 jit_solution(17589681722605825787)
XLA Ops:
  2.8 4.3 %all-to-all-start.1 = ((bf16[4,16,257]{2,1,0:T(8,128)(2,1)}), bf16[4,16,257]{2,1,0:T(8,128)(2,1)S(1)}, u32[]{:S(2)}, u32[]{:S(2)}) async-start(bf16[4,16,257]{2,1,0:T(8,128)(2,1)} %broadcast_in_dim.95), calls=%async_computation.1 | async-start | bytes 98304 | tf_op jit(solution)/shard_map/all_to_all | solution.py:37
  10.9 3.6 %fusion.13 = f32[336,4096]{1,0:T(8,128)S(1)} fusion(s32[32,8,32,128]{3,2,1,0:T(8,128)S(1)} %bitcast.154, bf16[32,8,32,128]{3,2,1,0:T(8,128)(2,1)S(1)} %bitcast.155, s32[256]{0:T(256)S(1)} %eq.76, bf16[112,256]{1,0:T(8,128)(2,1)S(1)} %get-tuple-element.223, bf16[112,256]{1,0:T(8,128)(2,1)S(1)} %get-tuple-element.222, bf16[112,256]{1,0:T(8,128)(2,1)S(1)} %get-tuple-element.224), kind=kOutput, calls=%fused_computation.26 | convolution fusion | flops 707256320 | bytes 11969536 | tf_op jit(solution)/shard_map/while/body/eval_jaxpr/dot_general | solution.py:150
  15.5 3.5 %divide_bitcast_fusion = (f32[32,112,128]{2,1,0:T(8,128)S(1)}, f32[32,112,128]{2,1,0:T(8,128)}) fusion(f32[14,32,8,128]{3,2,1,0:T(8,128)S(1)} %get-tuple-element.220, f32[32,128]{1,0:T(8,128)S(1)} %copy-done.4, f32[112]{0:T(128)S(1)} %copy-done.9, f32[32,128]{1,0:T(8,128)S(1)} %get-tuple-element.216, f32[32,128]{1,0:T(8,128)S(1)} %broadcast_multiply_fusion.2, ...), kind=kLoop, calls=%fused_computation.43 | loop fusion | flops 12845056 | bytes 9241024 | tf_op jit(solution)/shard_map/while/body/eval_jaxpr/transpose | solution.py:165
  20.4 47.5 %while.42 = (s32[]{:T(128)}, f32[112,128]{1,0:T(8,128)S(1)}, f32[32,112,128]{2,1,0:T(8,128)}, f32[32,112,128]{2,1,0:T(8,128)S(1)}, f32[32,112,128]{2,1,0:T(8,128)}, /*index=5*/s32[]{:T(128)}, s32[]{:T(128)}) while((s32[]{:T(128)}, f32[112,128]{1,0:T(8,128)S(1)}, f32[32,112,128]{2,1,0:T(8,128)}, f32[32,112,128]{2,1,0:T(8,128)S(1)}, ...), condition=%wide.region_1.2_spmd, body=%wide.region_0.1_spmd.sunk | while | flops 86019 | bytes 344161 | solution.py:180
  70.8 50.0 %while.43 = (s32[]{:T(128)}, f32[112,128]{1,0:T(8,128)S(1)}, f32[32,112,128]{2,1,0:T(8,128)S(1)}, f32[32,112,128]{2,1,0:T(8,128)}, f32[32,112,128]{2,1,0:T(8,128...) while((s32[]{:T(128)}, f32[112,128]{1,0:T(8,128)S(1)}, f32[32,112,128]{2,1,0:T(8,128)S(1)}, ...), condition=%wide.region_3.4_spmd, body=%wide.region_2.3_spmd.sunk | while | flops 71682 | bytes 459353 | solution.py:187
  70.8 1.6 bitcast_dynamic-update-slice_fusion.7
  75.5 1.5 bitcast_dynamic-update-slice_fusion.7
  80.2 1.5 bitcast_dynamic-update-slice_fusion.7
  81.7 1.5 bitcast_dynamic-update-slice_fusion.7
  88.0 1.5 bitcast_dynamic-update-slice_fusion.7
  92.7 1.5 bitcast_dynamic-update-slice_fusion.7
  94.2 1.5 bitcast_dynamic-update-slice_fusion.7
  95.8 1.5 bitcast_dynamic-update-slice_fusion.7
  102.0 1.5 bitcast_dynamic-update-slice_fusion.7
  106.7 1.5 bitcast_dynamic-update-slice_fusion.7
  108.3 1.6 bitcast_dynamic-update-slice_fusion.7
  117.6 1.5 bitcast_dynamic-update-slice_fusion.7
  119.2 1.5 bitcast_dynamic-update-slice_fusion.7
  120.8 1.6 slice.46
  125.8 29.5 %all_to_all.45 = bf16[128,2,385]{2,1,0:T(2,128)(2,1)S(1)} all-to-all(bf16[128,2,385]{2,1,0:T(2,128)(2,1)S(1)} %pad_maximum_fusion), channel_id=1, replica_groups=mesh['grp'=4,'lrn_0'=4,'lrn_1'=4,'lrn_2'=8] {'lrn_0','lrn_1','lrn_2'}, dimensions={0} | all-to-all | bytes 394240 | tf_op jit(solution)/shard_map/all_to_all | solution.py:24
  156.7 6.4 %all-to-all-start.2 = ((bf16[32,4,16,257]{3,2,1,0:T(8,128)(2,1)}), bf16[32,4,16,257]{3,2,1,0:T(8,128)(2,1)S(1)}, u32[]{:S(2)}, u32[]{:S(2)}) async-start(bf16[32,4,16,257]{3,2,1,0:T(8,128)(2,1)} %broadcast_in_dim.96), calls=%async_computation.2 | async-start | bytes 3145728 | tf_op jit(solution)/shard_map/all_to_all | solution.py:37
  163.5 36.8 %all-to-all-done.2 = bf16[32,4,16,257]{3,2,1,0:T(8,128)(2,1)S(1)} async-done(((bf16[32,4,16,257]{3,2,1,0:T(8,128)(2,1)}), bf16[32,4,16,257]{3,2,1,0:T(8,128)(2,1)S(1)}, u32[]{:S(2)}, u32[]{:S(2)}) %all-to-all-start.2) | async-done | bytes 1052704 | tf_op jit(solution)/shard_map/all_to_all | solution.py:37
  202.1 1.7 fusion.67
  205.4 45.8 %all_to_all.46 = bf16[32,4,16,257]{3,2,1,0:T(8,128)(2,1)S(1)} all-to-all(bf16[32,4,16,257]{3,2,1,0:T(8,128)(2,1)S(1)} %maximum_bitcast_fusion), channel_id=1, replica_groups=mesh['grp'=4,'lrn_0'=4,'lrn_1'=4,'lrn_2'=8] {'lrn_1','lrn_2'}, dimensions={0} | all-to-all | bytes 2105344 | tf_op jit(solution)/shard_map/all_to_all | solution.py:81
  252.1 4.6 %all-to-all-start.6 = ((bf16[4,16,257]{2,1,0:T(8,128)(2,1)}), bf16[4,16,257]{2,1,0:T(8,128)(2,1)S(1)}, u32[]{:S(2)}, u32[]{:S(2)}) async-start(bf16[4,16,257]{2,1,0:T(8,128)(2,1)} %reduce_sum.76), calls=%async_computation.6 | async-start | bytes 98304 | tf_op jit(solution)/shard_map/all_to_all | solution.py:89
  258.1 4.1 %all-to-all-done.6 = bf16[4,16,257]{2,1,0:T(8,128)(2,1)S(1)} async-done(((bf16[4,16,257]{2,1,0:T(8,128)(2,1)}), bf16[4,16,257]{2,1,0:T(8,128)(2,1)S(1)}, u32[]{:S(2)}, u32[]{:S(2)}) %all-to-all-start.6) | async-done | bytes 32928 | tf_op jit(solution)/shard_map/all_to_all | solution.py:89
  262.2 7.6 %all-to-all-start.3 = ((f32[4,512,128]{2,1,0:T(8,128)}), f32[4,512,128]{2,1,0:T(8,128)S(1)}, u32[]{:S(2)}, u32[]{:S(2)}) async-start(f32[4,512,128]{2,1,0:T(8,128)} %bitcast.24), calls=%async_computation.3 | async-start | bytes 2097152 | tf_op jit(solution)/shard_map/all_to_all | solution.py:71
  269.9 29.4 %all-to-all-done.3 = f32[4,512,128]{2,1,0:T(8,128)S(1)} async-done(((f32[4,512,128]{2,1,0:T(8,128)}), f32[4,512,128]{2,1,0:T(8,128)S(1)}, u32[]{:S(2)}, u32[]{:S(2)}) %all-to-all-start.3) | async-done | bytes 1048608 | tf_op jit(solution)/shard_map/all_to_all | solution.py:71
  300.0 3.3 all-to-all-start.7
  303.3 8.3 %all-to-all-done.7 = f32[4,1,4112]{2,1,0:T(1,128)S(1)} async-done(((f32[4,1,4112]{2,1,0:T(1,128)}), f32[4,1,4112]{2,1,0:T(1,128)S(1)}, u32[]{:S(2)}, u32[]{:S(2)}) %all-to-all-start.7) | async-done | bytes 65824 | tf_op jit(solution)/shard_map/all_to_all | solution.py:37
  312.6 3.5 %all-to-all-start.4 = ((f32[4,512,128]{2,1,0:T(8,128)}), f32[4,512,128]{2,1,0:T(8,128)S(1)}, u32[]{:S(2)}, u32[]{:S(2)}) async-start(f32[4,512,128]{2,1,0:T(8,128)} %broadcast_in_dim.97), calls=%async_computation.4 | async-start | bytes 2097152 | tf_op jit(solution)/shard_map/all_to_all | solution.py:37
  317.4 28.3 %all-to-all-done.4 = f32[4,512,128]{2,1,0:T(8,128)S(1)} async-done(((f32[4,512,128]{2,1,0:T(8,128)}), f32[4,512,128]{2,1,0:T(8,128)S(1)}, u32[]{:S(2)}, u32[]{:S(2)}) %all-to-all-start.4) | async-done | bytes 1048608 | tf_op jit(solution)/shard_map/all_to_all | solution.py:37
  (202 shorter events, 102.2 us)
Async XLA Ops:
  0.6 201.0 %copy-start = (bf16[1,2048,128]{2,1,0:T(8,128)(2,1)S(1)}, bf16[1,2048,128]{2,1,0:T(8,128)(2,1)}, u32[]{:S(2)}) copy-start(bf16[1,2048,128]{2,1,0:T(8,128)(2,1)} %param.37) | copy-start | bytes 1572868
  0.6 9.7 %copy-start.2 = (s32[4,32,128]{2,1,0:T(8,128)S(1)}, s32[4,32,128]{2,1,0:T(8,128)}, u32[]{:S(2)}) copy-start(s32[4,32,128]{2,1,0:T(8,128)} %param.22) | copy-start | bytes 196612
  2.8 123.0 %all-to-all-start.1 = ((bf16[4,16,257]{2,1,0:T(8,128)(2,1)}), bf16[4,16,257]{2,1,0:T(8,128)(2,1)S(1)}, u32[]{:S(2)}, u32[]{:S(2)}) async-start(bf16[4,16,257]{2,1,0:T(8,128)(2,1)} %broadcast_in_dim.95), calls=%async_computation.1 | async-start | bytes 98304 | tf_op jit(solution)/shard_map/all_to_all | solution.py:37
  14.5 0.7 copy-start.12
  14.5 0.7 copy-start.5
  14.5 0.7 copy-start.8
  14.5 0.7 copy-start.6
  14.5 1.0 copy-start.4
  14.6 1.0 copy-start.9
  19.1 50.1 %copy-start.10 = (f32[128]{0:T(128)S(1)}, f32[128]{0:T(128)}, u32[]{:S(2)}) copy-start(f32[128]{0:T(128)} %param.27) | copy-start | bytes 1540
  19.1 50.1 %copy-start.11 = (f32[112]{0:T(128)S(1)}, f32[112]{0:T(128)}, u32[]{:S(2)}) copy-start(f32[112]{0:T(128)} %param.32) | copy-start | bytes 1348
  67.9 1.2 copy-start.1
  122.4 2.0 copy-start.7
  124.4 32.4 %copy-start.3 = (f32[2,2,32,128]{3,2,1,0:T(8,128)}, f32[2,2,32,128]{3,2,1,0:T(8,128)S(1)}, u32[]{:S(2)}) copy-start(f32[2,2,32,128]{3,2,1,0:T(8,128)S(1)} %copy.64) | copy-start | bytes 196612
  156.7 43.6 %all-to-all-start.2 = ((bf16[32,4,16,257]{3,2,1,0:T(8,128)(2,1)}), bf16[32,4,16,257]{3,2,1,0:T(8,128)(2,1)S(1)}, u32[]{:S(2)}, u32[]{:S(2)}) async-start(bf16[32,4,16,257]{3,2,1,0:T(8,128)(2,1)} %broadcast_in_dim.96), calls=%async_computation.2 | async-start | bytes 3145728 | tf_op jit(solution)/shard_map/all_to_all | solution.py:37
  252.1 10.1 %all-to-all-start.6 = ((bf16[4,16,257]{2,1,0:T(8,128)(2,1)}), bf16[4,16,257]{2,1,0:T(8,128)(2,1)S(1)}, u32[]{:S(2)}, u32[]{:S(2)}) async-start(bf16[4,16,257]{2,1,0:T(8,128)(2,1)} %reduce_sum.76), calls=%async_computation.6 | async-start | bytes 98304 | tf_op jit(solution)/shard_map/all_to_all | solution.py:89
  262.2 37.1 %all-to-all-start.3 = ((f32[4,512,128]{2,1,0:T(8,128)}), f32[4,512,128]{2,1,0:T(8,128)S(1)}, u32[]{:S(2)}, u32[]{:S(2)}) async-start(f32[4,512,128]{2,1,0:T(8,128)} %bitcast.24), calls=%async_computation.3 | async-start | bytes 2097152 | tf_op jit(solution)/shard_map/all_to_all | solution.py:71
  300.0 11.6 %all-to-all-start.7 = ((f32[4,1,4112]{2,1,0:T(1,128)}), f32[4,1,4112]{2,1,0:T(1,128)S(1)}, u32[]{:S(2)}, u32[]{:S(2)}) async-start(f32[4,1,4112]{2,1,0:T(1,128)} %broadcast_in_dim.98), calls=%async_computation.7 | async-start | bytes 135168 | tf_op jit(solution)/shard_map/all_to_all | solution.py:37
  312.6 33.1 %all-to-all-start.4 = ((f32[4,512,128]{2,1,0:T(8,128)}), f32[4,512,128]{2,1,0:T(8,128)S(1)}, u32[]{:S(2)}, u32[]{:S(2)}) async-start(f32[4,512,128]{2,1,0:T(8,128)} %broadcast_in_dim.97), calls=%async_computation.4 | async-start | bytes 2097152 | tf_op jit(solution)/shard_map/all_to_all | solution.py:37
where the time goes:
time: 351 us; the launch traced here: 347 us
  waiting for transfers between devices  107 us (30%)
  other arithmetic  85.7 us (24%)
  blocking collectives  75.3 us (21%)
  local copies, waits for them, and re-layouts  35.9 us (10%)
  starting transfers between devices  29.7 us (8%)
  matrix products  11 us (3%)
    all_to_all x4, waiting for transfers between devices, from_everyone(): lax.all_to_all(jnp.broadcast_to(x[None], (devices, *x.shape)), axis, 0, 0...  73.4 us
    dynamic_update_slice x32, other arithmetic, column_block(): lax.scan(upward, surface, (reflect, transmit), reverse=True)  49.2 us
    all_to_all x1, blocking collectives, sent_and_summed_2(): lax.all_to_all(pieces, axis, split_axis=0, concat_axis=0, tiled=True)  45.8 us
    all_to_all x1, blocking collectives, in_one_piece(): lax.all_to_all(both, axis, split_axis=split_dim, concat_axis=concat_dim,...  29.5 us
    all_to_all x1, waiting for transfers between devices, sent_and_summed(): pieces = lax.all_to_all(in_blocks(x, dim, devices), axis, 0, 0, tiled=True)  29.4 us
    add x32, other arithmetic, upward(): layer_reflect + layer_transmit * layer_transmit * below_reflect / (1.0 -...  26.9 us
    dynamic_update_slice x64, local copies, waits for them, and re-layouts, column_block(): lax.scan(upward, surface, (reflect, transmit), reverse=True)  20.3 us
    all_to_all x4, starting transfers between devices, from_everyone(): lax.all_to_all(jnp.broadcast_to(x[None], (devices, *x.shape)), axis, 0, 0...  17.5 us
  transfers between devices with their start and end apart: 6, of which 5 were waited for; matrix products, arithmetic and copies ran while one was open for 34% of the time, Pallas kernels for 0%

commit v1 on v0

--- a/solution.py
+++ b/solution.py
@@ -5,8 +5,15 @@
 import jax.numpy as jnp
 from jax import lax
 from jax.sharding import Mesh
+from jax.experimental import pallas as pl
+from jax.experimental.pallas import tpu as pltpu
 from jax.sharding import PartitionSpec as P
 
+MODES = 4
+BINS = 64
+G = 112
+NB = 14
+LEV = 32
 COL_DEV = 128
 LRN = ("lrn_0", "lrn_1", "lrn_2")
 GRP_LRN = ("grp", "lrn_0", "lrn_1", "lrn_2")
@@ -14,7 +21,6 @@
 
 CLOUD_SSA = 0.99
 CLOUD_ASYM = 0.85
-PRECISE = lax.Precision.HIGHEST
 
 
 def in_one_piece(arrays, axis, split_dim, concat_dim, along):
@@ -117,137 +123,141 @@
     return tuple(gathered)
 
 
-def optics_table(ext_table, ssa_table, asym_table):
-    scatter = ext_table * ssa_table
-    return jnp.concatenate([ext_table, scatter, scatter * asym_table], axis=0).astype(jnp.bfloat16)
-
-
-def column_block(
-    optic_table,
-    gas_coeff,
-    solar_flux,
-    band_map,
-    aerosol_mass,
-    size_bins,
-    cloud_tau,
-    cloud_mask,
-    absorber,
-    surface_albedo,
-    cos_zenith,
-):
-    mode_count, levels, width_cols = aerosol_mass.shape
-    point_count = gas_coeff.shape[0]
-    bin_count = optic_table.shape[1] // mode_count
-    band_count = surface_albedo.shape[0]
-    labels = jnp.arange(bin_count, dtype=jnp.int32)
-    load_bf = aerosol_mass.astype(jnp.bfloat16)
-    weights = jnp.where(
-        size_bins[:, None] == labels[None, :, None, None],
-        load_bf[:, None],
-        jnp.zeros((), jnp.bfloat16),
-    )
-    weights = weights.reshape(mode_count * bin_count, levels * width_cols)
-    optics = jnp.dot(optic_table, weights, preferred_element_type=jnp.float32).reshape(
-        3, point_count, levels, width_cols
-    )
-    cloudy = (cloud_tau * cloud_mask.astype(jnp.float32)[None, :])[None]
-    optical_depth = optics[0] + cloudy + gas_coeff[:, None, None] * absorber[None]
-    scatter = optics[1] + CLOUD_SSA * cloudy
-    forward = optics[2] + CLOUD_SSA * CLOUD_ASYM * cloudy
-    single_albedo = scatter / optical_depth
-    asym_factor = forward / scatter
-    gamma_one = 2.0 - single_albedo * (1.0 + asym_factor)
-    gamma_two = single_albedo * (1.0 - asym_factor)
-    decay_rate = jnp.sqrt((gamma_one - gamma_two) * (gamma_one + gamma_two))
-    damped = jnp.exp(-decay_rate * optical_depth)
-    square = damped * damped
-    denominator = decay_rate + gamma_one + (decay_rate - gamma_one) * square
-    reflect = jnp.moveaxis(gamma_two * (1.0 - square) / denominator, 1, 0)
-    transmit = jnp.moveaxis(2.0 * decay_rate * damped / denominator, 1, 0)
-    band_hot = (band_map[:, None] == jnp.arange(band_count, dtype=jnp.int32)[None, :]).astype(
-        jnp.float32
-    )
-    surface = jnp.dot(band_hot, surface_albedo, precision=PRECISE)
-    source = solar_flux[:, None] * cos_zenith[None, :]
-
-    def upward(below_reflect, layer):
-        layer_reflect, layer_transmit = layer
-        above = layer_reflect + layer_transmit * layer_transmit * below_reflect / (
-            1.0 - layer_reflect * below_reflect
-        )
-        return (above, below_reflect)
-
-    top_reflect, below_all = lax.scan(upward, surface, (reflect, transmit), reverse=True)
-
-    def downward(down_now, layer):
-        layer_reflect, layer_transmit, below_reflect = layer
-        down_next = layer_transmit * down_now / (1.0 - layer_reflect * below_reflect)
-        return (down_next, (down_next, below_reflect * down_next))
-
-    _, (down_all, up_all) = lax.scan(downward, source, (reflect, transmit, below_all))
-    upper = jnp.concatenate([(top_reflect * source)[None], up_all[:-1]], axis=0)
-    group_hot = jnp.stack([band_map < band_count // 2, band_map >= band_count // 2]).astype(
-        jnp.float32
-    ) * (2.0 / point_count)
-    down_flux = jnp.einsum("kg,lgc->klc", group_hot, down_all, precision=PRECISE)
-    up_flux = jnp.einsum("kg,lgc->klc", group_hot, upper, precision=PRECISE)
-    return jnp.stack([down_flux, up_flux], axis=1).reshape(4 * levels, width_cols)
-
-
-def evolve(
-    optic_table,
-    gas_coeff,
-    solar_flux,
-    band_map,
-    aerosol_mass,
-    size_bins,
-    cloud_tau,
-    cloud_mask,
-    absorber,
-    surface_albedo,
-    cos_zenith,
-):
-    total_cols = aerosol_mass.shape[-1]
-    block_size = min(total_cols, 256)
-    block_count = total_cols // block_size
-
-    def splitter(array_in):
-        return jnp.moveaxis(
-            array_in.reshape(array_in.shape[:-1] + (block_count, block_size)), -2, 0
-        )
-
-    pieces = tuple(
-        (
-            splitter(array_in)
-            for array_in in (
-                aerosol_mass,
-                size_bins,
-                cloud_tau,
-                cloud_mask,
-                absorber,
-                surface_albedo,
-                cos_zenith,
-            )
-        )
-    )
-
-    def column_job(piece):
-        return column_block(
-            optic_table,
-            gas_coeff,
-            solar_flux,
-            band_map,
-            piece[0],
-            piece[1],
-            piece[2],
-            piece[3],
-            piece[4],
-            piece[5],
-            piece[6],
-        )
-
-    results = lax.map(column_job, pieces)
-    return jnp.moveaxis(results, 0, 1).reshape(results.shape[1], total_cols)
+def row_to_col(row):
+    n = row.shape[1]
+    rows = lax.broadcasted_iota(jnp.int32, (n, n), 0)
+    cols = lax.broadcasted_iota(jnp.int32, (n, n), 1)
+    return jnp.sum(jnp.where(rows == cols, jnp.broadcast_to(row, (n, n)), 0.0), axis=1, keepdims=True)
+
+
+def evolve_setup(ext, ssa, asy, gas, sol, band, tab, gcol, m0):
+    e = ext[...]
+    s = e * ssa[...]
+    tab[0:G, :] = e.astype(jnp.bfloat16)
+    tab[G : 2 * G, :] = s.astype(jnp.bfloat16)
+    tab[2 * G : 3 * G, :] = (s * asy[...]).astype(jnp.bfloat16)
+    gcol[...] = jnp.broadcast_to(row_to_col(gas[...]), (G, COL_DEV))
+    bcol = row_to_col(band[...].astype(jnp.float32))
+    m0[...] = jnp.broadcast_to(jnp.where(bcol < NB // 2, 1.0, 0.0), (G, COL_DEV))
+    return bcol
+
+
+CH = 8
+LU = 4
+
+
+def evolve_layers(mass, bins, tau, mask, absb, tab, gcol, opt, refl, trans):
+    labels = lax.broadcasted_iota(jnp.int32, (BINS, COL_DEV), 0)
+    cloudy_on = mask[...].astype(jnp.float32)
+
+    def body(step, carry):
+        pieces = []
+        for u in range(LU):
+            l = step * LU + u
+            modes = []
+            for m in range(MODES):
+                load = mass[m, pl.ds(l, 1), :]
+                hot = bins[m, pl.ds(l, 1), :] == labels
+                modes.append(jnp.where(hot, jnp.broadcast_to(load, (BINS, COL_DEV)), 0.0))
+            pieces.append(jnp.concatenate(modes, axis=0).astype(jnp.bfloat16))
+        weights = jnp.concatenate(pieces, axis=1)
+        opt[...] = jnp.dot(tab[...], weights, preferred_element_type=jnp.float32)
+        for u in range(LU):
+            l = step * LU + u
+            cl = tau[pl.ds(l, 1), :] * cloudy_on
+            ab = absb[pl.ds(l, 1), :]
+            c1 = CLOUD_SSA * cl
+            c2 = CLOUD_SSA * CLOUD_ASYM * cl
+            lanes = slice(u * COL_DEV, (u + 1) * COL_DEV)
+            for g in range(0, G, CH):
+                d = opt[g : g + CH, lanes] + cl + gcol[g : g + CH, :] * ab
+                s = opt[G + g : G + g + CH, lanes] + c1
+                f = opt[2 * G + g : 2 * G + g + CH, lanes] + c2
+                ds, df = d - s, d - f
+                k = 2.0 * jnp.sqrt(ds * df)
+                g1 = ds + df
+                e = jnp.exp(-k)
+                sq = e * e
+                r = 1.0 / ((k + g1) + (k - g1) * sq)
+                refl[l, g : g + CH, :] = (s - f) * (1.0 - sq) * r
+                trans[l, g : g + CH, :] = 2.0 * k * e * r
+        return carry
+
+    lax.fori_loop(0, LEV // LU, body, 0)
+
+
+def evolve_up(alb, bcol, refl, trans, below):
+    surface = jnp.zeros((G, COL_DEV), jnp.float32)
+    for b in range(NB):
+        surface = jnp.where(bcol == float(b), jnp.broadcast_to(alb[b : b + 1, :], (G, COL_DEV)), surface)
+    below[LEV] = surface
+
+    def body(step, carry):
+        l = LEV - 1 - step
+        for g in range(0, G, CH):
+            rows = slice(g, g + CH)
+            b = below[l + 1, rows, :]
+            r = refl[l, rows, :]
+            t = trans[l, rows, :]
+            q = t / (1.0 - r * b)
+            below[l, rows, :] = r + t * b * q
+            trans[l, rows, :] = q
+        return carry
+
+    lax.fori_loop(0, LEV, body, 0)
+
+
+def evolve_down(sol, cosz, m0, below, trans, down, flux):
+    cosv = cosz[...]
+    scol = row_to_col(sol[...])
+    down[...] = jnp.broadcast_to(scol, (G, COL_DEV)) * cosv
+    scale = 2.0 / G
+
+    def body(l, carry):
+        acc = [jnp.zeros((CH, COL_DEV), jnp.float32) for _ in range(4)]
+        for g in range(0, G, CH):
+            rows = slice(g, g + CH)
+            now = down[rows, :]
+            low = m0[rows, :]
+            up = below[l, rows, :] * now
+            nxt = trans[l, rows, :] * now
+            down[rows, :] = nxt
+            nl, ul = nxt * low, up * low
+            acc[0] = acc[0] + nl
+            acc[1] = acc[1] + ul
+            acc[2] = acc[2] + (nxt - nl)
+            acc[3] = acc[3] + (up - ul)
+        for i in range(4):
+            flux[pl.ds(i * LEV + l, 1), :] = jnp.sum(acc[i], axis=0, keepdims=True) * scale
+        return carry
+
+    lax.fori_loop(0, LEV, body, 0)
+
+
+def evolve_kernel(mass, bins, tau, mask, absb, alb, cosz, ext, ssa, asy, gas, sol, band, flux,
+                  tab, gcol, m0, opt, refl, trans, below, down):
+    bcol = evolve_setup(ext, ssa, asy, gas, sol, band, tab, gcol, m0)
+    evolve_layers(mass, bins, tau, mask, absb, tab, gcol, opt, refl, trans)
+    evolve_up(alb, bcol, refl, trans, below)
+    evolve_down(sol, cosz, m0, below, trans, down, flux)
+
+
+def evolve(mass, bins, tau, mask, absb, alb, cosz, ext, ssa, asy, gas, sol, band):
+    return pl.pallas_call(
+        evolve_kernel,
+        out_shape=jax.ShapeDtypeStruct((4 * LEV, COL_DEV), jnp.float32),
+        scratch_shapes=[
+            pltpu.VMEM((3 * G, MODES * BINS), jnp.bfloat16),
+            pltpu.VMEM((G, COL_DEV), jnp.float32),
+            pltpu.VMEM((G, COL_DEV), jnp.float32),
+            pltpu.VMEM((3 * G, LU * COL_DEV), jnp.float32),
+            pltpu.VMEM((LEV, G, COL_DEV), jnp.float32),
+            pltpu.VMEM((LEV, G, COL_DEV), jnp.float32),
+            pltpu.VMEM((LEV + 1, G, COL_DEV), jnp.float32),
+            pltpu.VMEM((G, COL_DEV), jnp.float32),
+        ],
+        cost_estimate=pl.CostEstimate(flops=10**9, bytes_accessed=10**6, transcendentals=10**6),
+    )(mass, bins, tau, mask[None], absb, alb, cosz[None], ext, ssa, asy, gas[None], sol[None], band[None])
 
 
 def column_features(aerosol_mass, size_bins, bin_count):
@@ -302,12 +312,7 @@
     trunk_bias,
     head_weight,
 ):
-    optic_table = optics_table(ext_table, ssa_table, asym_table)
     fluxes = evolve(
-        optic_table,
-        gas_coeff,
-        solar_flux,
-        band_map,
         aerosol_mass,
         size_bins,
         cloud_tau,
@@ -315,9 +320,15 @@
         absorber,
         surface_albedo,
         cos_zenith,
+        ext_table,
+        ssa_table,
+        asym_table,
+        gas_coeff,
+        solar_flux,
+        band_map,
     )
     features = column_features(
-        aerosol_mass, size_bins, optic_table.shape[1] // aerosol_mass.shape[0]
+        aerosol_mass, size_bins, BINS
     )
     targets = fluxes.astype(jnp.bfloat16)
     columns_here = aerosol_mass.shape[-1]

time: 351 us -> 247 us (0.70)
  other arithmetic: 85.7 us -> 7.61 us
  local copies, waits for them, and re-layouts: 35.9 us -> 8.36 us
  Pallas kernels: 0 us -> 12.1 us
  matrix products: 11 us -> 5.24 us
    dynamic_update_slice x32 -> x0, other arithmetic: 49.2 us -> none  [column_block(): lax.scan(upward, surface, (reflect, transmit), reverse=True)]
    add x32 -> x0, other arithmetic: 26.9 us -> none  [upward(): layer_reflect + layer_transmit * layer_transmit * below_reflect / (1.0 -...]
    dynamic_update_slice x64 -> x0, local copies, waits for them, and re-layouts: 20.3 us -> none  [column_block(): lax.scan(upward, surface, (reflect, transmit), reverse=True)]
    pallas_call x0 -> x1, Pallas kernels: none -> 12.1 us  [evolve(): pl.pallas_call(evolve_kernel, out_shape=jax.ShapeDtypeStruct((4 * LEV, CO...]
    dot_general x4 -> x0, matrix products: 5.74 us -> none  [the longest x1 3.57 us: column_block(): jnp.dot(optic_table, weights, preferred_element_type=jnp.float32)]
    transpose x1 -> x0, other arithmetic: 3.54 us -> none  [column_block(): reflect = jnp.moveaxis(gamma_two * (1.0 - square) / denominator, 1, 0)]
  transfers between devices with their start and end apart: 6 -> 6, of which waited for: 5 -> 5; matrix products, arithmetic and copies ran while one was open for 34% -> 4% of each run, Pallas kernels for 0% -> 5%
where the time goes in v1:
time: 247 us; the launch traced here: 246 us
  waiting for transfers between devices  107 us (43%)
  blocking collectives  75.4 us (31%)
  starting transfers between devices  29.5 us (12%)
  Pallas kernels  12.1 us (5%)
  local copies, waits for them, and re-layouts  8.36 us (3%)
  other arithmetic  7.61 us (3%)
  matrix products  5.24 us (2%)
    all_to_all x4, waiting for transfers between devices, from_everyone(): lax.all_to_all(jnp.broadcast_to(x[None], (devices, *x.shape)), axis, 0, 0...  73.4 us
    all_to_all x1, blocking collectives, sent_and_summed_2(): lax.all_to_all(pieces, axis, split_axis=0, concat_axis=0, tiled=True)  45.9 us
    all_to_all x1, blocking collectives, in_one_piece(): lax.all_to_all(both, axis, split_axis=split_dim, concat_axis=concat_dim,...  29.5 us
    all_to_all x1, waiting for transfers between devices, sent_and_summed(): pieces = lax.all_to_all(in_blocks(x, dim, devices), axis, 0, 0, tiled=True)  29.4 us
    all_to_all x4, starting transfers between devices, from_everyone(): lax.all_to_all(jnp.broadcast_to(x[None], (devices, *x.shape)), axis, 0, 0...  17.5 us
    pallas_call x1, Pallas kernels, evolve(): pl.pallas_call(evolve_kernel, out_shape=jax.ShapeDtypeStruct((4 * LEV, CO...  12.1 us
    all_to_all x1, starting transfers between devices, sent_and_summed(): pieces = lax.all_to_all(in_blocks(x, dim, devices), axis, 0, 0, tiled=True)  7.57 us
  transfers between devices with their start and end apart: 6, of which 5 were waited for; matrix products, arithmetic and copies ran while one was open for 4% of the time, Pallas kernels for 5%

profile of v1, /device:TPU:64, one launch (start us, length us, event | category | flops | bytes accessed | tf_op | source)
XLA Modules:
  0.0 245.9 jit_solution(12855403289326144532)
XLA Ops:
  0.6 0.8 copy.43
  1.4 0.7 pad_maximum_fusion.2
  2.2 0.6 broadcast_in_dim.23
  2.8 4.3 %all-to-all-start.1 = ((bf16[4,16,257]{2,1,0:T(8,128)(2,1)}), bf16[4,16,257]{2,1,0:T(8,128)(2,1)S(1)}, u32[]{:S(2)}, u32[]{:S(2)}) async-start(bf16[4,16,257]{2,1,0:T(8,128)(2,1)} %broadcast_in_dim.23), calls=%async_computation.1 | async-start | bytes 98304 | tf_op jit(solution)/shard_map/all_to_all | solution.py:43
  7.1 0.7 fusion.23
  8.0 0.8 select_reduce_fusion
  8.8 0.7 multiply_add_fusion
  9.5 0.9 multiply_convert_fusion.2
  10.3 0.9 multiply_convert_fusion.1
  11.2 12.1 %shard_map.192 = f32[128,128]{1,0:T(8,128)} custom-call(f32[4,32,128]{2,1,0:T(8,128)} %mass.1, s32[4,32,128]{2,1,0:T(8,128)} %bins.1, f32[32,128]{1,0:T(8,128)} %tau.1, s32[1,128]{1,0:T(1,128)} %bitcast.43, f32[32,128]{1,0:T(8,128)} %absb.1, f32[14,128]{1,0:T(8,128)} %alb.1, f32[1,128]{1,0:T(1,128)} %bitcast.44, f32[112,256]{1,0:T(8,128)} %ext.1, ...), custom_call_target="tpu_custom_call" | custom-call | flops 1000000000 | bytes 1000000 | tf_op jit(solution)/shard_map/pallas_call | solution.py:246
  23.3 0.8 convert_element_type.54
  25.1 29.5 %all_to_all.45 = bf16[128,2,385]{2,1,0:T(2,128)(2,1)S(1)} all-to-all(bf16[128,2,385]{2,1,0:T(2,128)(2,1)S(1)} %pad_maximum_fusion), channel_id=1, replica_groups=mesh['grp'=4,'lrn_0'=4,'lrn_1'=4,'lrn_2'=8] {'lrn_0','lrn_1','lrn_2'}, dimensions={0} | all-to-all | bytes 394240 | tf_op jit(solution)/shard_map/all_to_all | solution.py:30
  54.6 1.4 broadcast_in_dim.24
  56.0 6.4 %all-to-all-start.2 = ((bf16[32,4,16,257]{3,2,1,0:T(8,128)(2,1)}), bf16[32,4,16,257]{3,2,1,0:T(8,128)(2,1)S(1)}, u32[]{:S(2)}, u32[]{:S(2)}) async-start(bf16[32,4,16,257]{3,2,1,0:T(8,128)(2,1)} %broadcast_in_dim.24), calls=%async_computation.2 | async-start | bytes 3145728 | tf_op jit(solution)/shard_map/all_to_all | solution.py:43
  62.8 36.9 %all-to-all-done.2 = bf16[32,4,16,257]{3,2,1,0:T(8,128)(2,1)S(1)} async-done(((bf16[32,4,16,257]{3,2,1,0:T(8,128)(2,1)}), bf16[32,4,16,257]{3,2,1,0:T(8,128)(2,1)S(1)}, u32[]{:S(2)}, u32[]{:S(2)}) %all-to-all-start.2) | async-done | bytes 1052704 | tf_op jit(solution)/shard_map/all_to_all | solution.py:43
  100.0 1.0 multiply_convert_fusion
  101.4 1.7 fusion.25
  103.7 0.8 copy.46
  104.7 45.9 %all_to_all.46 = bf16[32,4,16,257]{3,2,1,0:T(8,128)(2,1)S(1)} all-to-all(bf16[32,4,16,257]{3,2,1,0:T(8,128)(2,1)S(1)} %maximum_bitcast_fusion), channel_id=1, replica_groups=mesh['grp'=4,'lrn_0'=4,'lrn_1'=4,'lrn_2'=8] {'lrn_1','lrn_2'}, dimensions={0} | all-to-all | bytes 2105344 | tf_op jit(solution)/shard_map/all_to_all | solution.py:87
  150.6 0.9 reduce_sum.76
  151.5 4.4 %all-to-all-start.6 = ((bf16[4,16,257]{2,1,0:T(8,128)(2,1)}), bf16[4,16,257]{2,1,0:T(8,128)(2,1)S(1)}, u32[]{:S(2)}, u32[]{:S(2)}) async-start(bf16[4,16,257]{2,1,0:T(8,128)(2,1)} %reduce_sum.76), calls=%async_computation.6 | async-start | bytes 98304 | tf_op jit(solution)/shard_map/all_to_all | solution.py:95
  155.9 1.5 fusion.26
  157.3 4.1 %all-to-all-done.6 = bf16[4,16,257]{2,1,0:T(8,128)(2,1)S(1)} async-done(((bf16[4,16,257]{2,1,0:T(8,128)(2,1)}), bf16[4,16,257]{2,1,0:T(8,128)(2,1)S(1)}, u32[]{:S(2)}, u32[]{:S(2)}) %all-to-all-start.6) | async-done | bytes 32928 | tf_op jit(solution)/shard_map/all_to_all | solution.py:95
  161.4 7.6 %all-to-all-start.3 = ((f32[4,512,128]{2,1,0:T(8,128)}), f32[4,512,128]{2,1,0:T(8,128)S(1)}, u32[]{:S(2)}, u32[]{:S(2)}) async-start(f32[4,512,128]{2,1,0:T(8,128)} %bitcast.12), calls=%async_computation.3 | async-start | bytes 2097152 | tf_op jit(solution)/shard_map/all_to_all | solution.py:77
  169.1 29.4 %all-to-all-done.3 = f32[4,512,128]{2,1,0:T(8,128)S(1)} async-done(((f32[4,512,128]{2,1,0:T(8,128)}), f32[4,512,128]{2,1,0:T(8,128)S(1)}, u32[]{:S(2)}, u32[]{:S(2)}) %all-to-all-start.3) | async-done | bytes 1048608 | tf_op jit(solution)/shard_map/all_to_all | solution.py:77
  198.5 0.7 broadcast_in_dim.52
  199.2 3.3 %all-to-all-start.7 = ((f32[4,1,4112]{2,1,0:T(1,128)}), f32[4,1,4112]{2,1,0:T(1,128)S(1)}, u32[]{:S(2)}, u32[]{:S(2)}) async-start(f32[4,1,4112]{2,1,0:T(1,128)} %broadcast_in_dim.52), calls=%async_computation.7 | async-start | bytes 135168 | tf_op jit(solution)/shard_map/all_to_all | solution.py:43
  202.6 8.3 %all-to-all-done.7 = f32[4,1,4112]{2,1,0:T(1,128)S(1)} async-done(((f32[4,1,4112]{2,1,0:T(1,128)}), f32[4,1,4112]{2,1,0:T(1,128)S(1)}, u32[]{:S(2)}, u32[]{:S(2)}) %all-to-all-start.7) | async-done | bytes 65824 | tf_op jit(solution)/shard_map/all_to_all | solution.py:43
  210.8 1.0 broadcast_in_dim.25
  211.8 3.5 %all-to-all-start.4 = ((f32[4,512,128]{2,1,0:T(8,128)}), f32[4,512,128]{2,1,0:T(8,128)S(1)}, u32[]{:S(2)}, u32[]{:S(2)}) async-start(f32[4,512,128]{2,1,0:T(8,128)} %broadcast_in_dim.25), calls=%async_computation.4 | async-start | bytes 2097152 | tf_op jit(solution)/shard_map/all_to_all | solution.py:43
  216.6 28.3 %all-to-all-done.4 = f32[4,512,128]{2,1,0:T(8,128)S(1)} async-done(((f32[4,512,128]{2,1,0:T(8,128)}), f32[4,512,128]{2,1,0:T(8,128)S(1)}, u32[]{:S(2)}, u32[]{:S(2)}) %all-to-all-start.4) | async-done | bytes 1048608 | tf_op jit(solution)/shard_map/all_to_all | solution.py:43
  244.9 1.0 copy.55
  (27 shorter events, 4.4 us)
Async XLA Ops:
  0.6 100.3 %copy-start = (bf16[1,2048,128]{2,1,0:T(8,128)(2,1)S(1)}, bf16[1,2048,128]{2,1,0:T(8,128)(2,1)}, u32[]{:S(2)}) copy-start(bf16[1,2048,128]{2,1,0:T(8,128)(2,1)} %param.33) | copy-start | bytes 1572868
  2.8 22.3 %all-to-all-start.1 = ((bf16[4,16,257]{2,1,0:T(8,128)(2,1)}), bf16[4,16,257]{2,1,0:T(8,128)(2,1)S(1)}, u32[]{:S(2)}, u32[]{:S(2)}) async-start(bf16[4,16,257]{2,1,0:T(8,128)(2,1)} %broadcast_in_dim.23), calls=%async_computation.1 | async-start | bytes 98304 | tf_op jit(solution)/shard_map/all_to_all | solution.py:43
  56.0 43.6 %all-to-all-start.2 = ((bf16[32,4,16,257]{3,2,1,0:T(8,128)(2,1)}), bf16[32,4,16,257]{3,2,1,0:T(8,128)(2,1)S(1)}, u32[]{:S(2)}, u32[]{:S(2)}) async-start(bf16[32,4,16,257]{3,2,1,0:T(8,128)(2,1)} %broadcast_in_dim.24), calls=%async_computation.2 | async-start | bytes 3145728 | tf_op jit(solution)/shard_map/all_to_all | solution.py:43
  151.5 9.9 %all-to-all-start.6 = ((bf16[4,16,257]{2,1,0:T(8,128)(2,1)}), bf16[4,16,257]{2,1,0:T(8,128)(2,1)S(1)}, u32[]{:S(2)}, u32[]{:S(2)}) async-start(bf16[4,16,257]{2,1,0:T(8,128)(2,1)} %reduce_sum.76), calls=%async_computation.6 | async-start | bytes 98304 | tf_op jit(solution)/shard_map/all_to_all | solution.py:95
  161.4 37.1 %all-to-all-start.3 = ((f32[4,512,128]{2,1,0:T(8,128)}), f32[4,512,128]{2,1,0:T(8,128)S(1)}, u32[]{:S(2)}, u32[]{:S(2)}) async-start(f32[4,512,128]{2,1,0:T(8,128)} %bitcast.12), calls=%async_computation.3 | async-start | bytes 2097152 | tf_op jit(solution)/shard_map/all_to_all | solution.py:77
  199.2 11.6 %all-to-all-start.7 = ((f32[4,1,4112]{2,1,0:T(1,128)}), f32[4,1,4112]{2,1,0:T(1,128)S(1)}, u32[]{:S(2)}, u32[]{:S(2)}) async-start(f32[4,1,4112]{2,1,0:T(1,128)} %broadcast_in_dim.52), calls=%async_computation.7 | async-start | bytes 135168 | tf_op jit(solution)/shard_map/all_to_all | solution.py:43
  211.8 33.1 %all-to-all-start.4 = ((f32[4,512,128]{2,1,0:T(8,128)}), f32[4,512,128]{2,1,0:T(8,128)S(1)}, u32[]{:S(2)}, u32[]{:S(2)}) async-start(f32[4,512,128]{2,1,0:T(8,128)} %broadcast_in_dim.25), calls=%async_computation.4 | async-start | bytes 2097152 | tf_op jit(solution)/shard_map/all_to_all | solution.py:43

commit v2 on v1

v2 whole, which is shorter than its diff:
```python
import math

import jax
import jax.numpy as jnp
from jax import lax
from jax.experimental import pallas as pl
from jax.experimental.pallas import tpu as pltpu
from jax.sharding import Mesh
from jax.sharding import PartitionSpec as P

MODES = 4
BINS = 64
G = 112
NB = 14
LEV = 32
COL_DEV = 128
LRN = ("x", "zl", "y")
GRP_LRN = ("zh", "cc", "x", "zl", "y")
MESH = pl.DeviceIdType.MESH
BF = jnp.bfloat16
F32 = jnp.float32
CLOUD_SSA = 0.99
CLOUD_ASYM = 0.85


def nt(a, b):
    return lax.dot_general(a, b, (((1,), (1,)), ((), ())), preferred_element_type=F32)


def nn(a, b):
    return jnp.dot(a, b, preferred_element_type=F32)


def iota(shape, dim):
    return lax.broadcasted_iota(jnp.int32, shape, dim)


def row_to_col(row):
    n = row.shape[1]
    rows = lax.broadcasted_iota(jnp.int32, (n, n), 0)
    cols = lax.broadcasted_iota(jnp.int32, (n, n), 1)
    return jnp.sum(jnp.where(rows == cols, jnp.broadcast_to(row, (n, n)), 0.0), axis=1, keepdims=True)


def evolve_setup(ext, ssa, asy, gas, sol, band, tab, gcol, m0):
    e = ext[...]
    s = e * ssa[...]
    tab[0:G, :] = e.astype(jnp.bfloat16)
    tab[G : 2 * G, :] = s.astype(jnp.bfloat16)
    tab[2 * G : 3 * G, :] = (s * asy[...]).astype(jnp.bfloat16)
    gcol[...] = jnp.broadcast_to(row_to_col(gas[...]), (G, COL_DEV))
    bcol = row_to_col(band[...].astype(jnp.float32))
    m0[...] = jnp.broadcast_to(jnp.where(bcol < NB // 2, 1.0, 0.0), (G, COL_DEV))
    return bcol


CH = 8
LU = 4


def evolve_layers(mass, bins, tau, mask, absb, tab, gcol, opt, refl, trans):
    labels = lax.broadcasted_iota(jnp.int32, (BINS, COL_DEV), 0)
    cloudy_on = mask[...].astype(jnp.float32)

    def body(step, carry):
        pieces = []
        for u in range(LU):
            l = step * LU + u
            modes = []
            for m in range(MODES):
                load = mass[m, pl.ds(l, 1), :]
                hot = bins[m, pl.ds(l, 1), :] == labels
                modes.append(jnp.where(hot, jnp.broadcast_to(load, (BINS, COL_DEV)), 0.0))
            pieces.append(jnp.concatenate(modes, axis=0).astype(jnp.bfloat16))
        weights = jnp.concatenate(pieces, axis=1)
        opt[...] = jnp.dot(tab[...], weights, preferred_element_type=jnp.float32)
        for u in range(LU):
            l = step * LU + u
            cl = tau[pl.ds(l, 1), :] * cloudy_on
            ab = absb[pl.ds(l, 1), :]
            c1 = CLOUD_SSA * cl
            c2 = CLOUD_SSA * CLOUD_ASYM * cl
            lanes = slice(u * COL_DEV, (u + 1) * COL_DEV)
            for g in range(0, G, CH):
                d = opt[g : g + CH, lanes] + cl + gcol[g : g + CH, :] * ab
                s = opt[G + g : G + g + CH, lanes] + c1
                f = opt[2 * G + g : 2 * G + g + CH, lanes] + c2
                ds, df = d - s, d - f
                k = 2.0 * jnp.sqrt(ds * df)
                g1 = ds + df
                e = jnp.exp(-k)
                sq = e * e
                r = 1.0 / ((k + g1) + (k - g1) * sq)
                refl[l, g : g + CH, :] = (s - f) * (1.0 - sq) * r
                trans[l, g : g + CH, :] = 2.0 * k * e * r
        return carry

    lax.fori_loop(0, LEV // LU, body, 0)


def evolve_up(alb, bcol, refl, trans, below):
    surface = jnp.zeros((G, COL_DEV), jnp.float32)
    for b in range(NB):
        surface = jnp.where(bcol == float(b), jnp.broadcast_to(alb[b : b + 1, :], (G, COL_DEV)), surface)
    below[LEV] = surface

    def body(step, carry):
        l = LEV - 1 - step
        for g in range(0, G, CH):
            rows = slice(g, g + CH)
            b = below[l + 1, rows, :]
            r = refl[l, rows, :]
            t = trans[l, rows, :]
            q = t / (1.0 - r * b)
            below[l, rows, :] = r + t * b * q
            trans[l, rows, :] = q
        return carry

    lax.fori_loop(0, LEV, body, 0)


def evolve_down(sol, cosz, m0, below, trans, down, flux):
    cosv = cosz[...]
    scol = row_to_col(sol[...])
    down[...] = jnp.broadcast_to(scol, (G, COL_DEV)) * cosv
    scale = 2.0 / G

    def body(l, carry):
        acc = [jnp.zeros((CH, COL_DEV), jnp.float32) for _ in range(4)]
        for g in range(0, G, CH):
            rows = slice(g, g + CH)
            now = down[rows, :]
            low = m0[rows, :]
            up = below[l, rows, :] * now
            nxt = trans[l, rows, :] * now
            down[rows, :] = nxt
            nl, ul = nxt * low, up * low
            acc[0] = acc[0] + nl
            acc[1] = acc[1] + ul
            acc[2] = acc[2] + (nxt - nl)
            acc[3] = acc[3] + (up - ul)
        for i in range(4):
            flux[pl.ds(i * LEV + l, 1), :] = jnp.sum(acc[i], axis=0, keepdims=True) * scale
        return carry

    lax.fori_loop(0, LEV, body, 0)


EMPTY = 2.0
ROOT = math.sqrt(2.0 / math.pi)
CUBE = 0.044715


def remote(src, dst, send, recv, **at):
    return pltpu.make_async_remote_copy(
        src_ref=src, dst_ref=dst, send_sem=send, recv_sem=recv, device_id=at, device_id_type=MESH
    )


def wait_bytes(ref, sem):
    pltpu.make_async_copy(ref, ref, sem).wait()


def send_features(mass, bins, lr, fs, slot_col):
    row = lr[...]
    col = row_to_col(row.astype(F32))
    same = jnp.broadcast_to(col, (COL_DEV, COL_DEV)) == jnp.broadcast_to(row.astype(F32), (COL_DEV, COL_DEV))
    before = iota((COL_DEV, COL_DEV), 0) < iota((COL_DEV, COL_DEV), 1)
    rank = jnp.sum(jnp.where(same & before, 1.0, 0.0), axis=0, keepdims=True).astype(jnp.int32)
    peer = (row >> 5) * 8 + (row & 7)
    key = peer * 16 + ((row >> 3) & 3) * 4 + rank
    slot_col[...] = peer * 8 + ((row >> 3) & 3) * 2 + rank
    first = ((jnp.log(mass[...]) + 4.6) / 1.4).reshape(MODES * LEV, COL_DEV).astype(BF)
    half = BINS / 2
    second = ((bins[...].astype(F32) - half) / half).reshape(MODES * LEV, COL_DEV).astype(BF)
    rows = iota((512, COL_DEV), 0)
    hot0 = jnp.where(rows == key, 1.0, 0.0).astype(BF)
    hot1 = jnp.where(rows == key + 2, 1.0, 0.0).astype(BF)
    data = nt(hot0, first) + nt(hot1, second)
    filled = nn(hot0 + hot1, jnp.ones((COL_DEV, COL_DEV), BF))
    empty = (filled < 0.5) & (iota((512, COL_DEV), 1) == 0)
    fs[...] = jnp.where(empty, EMPTY, data).reshape(32, 16, COL_DEV).astype(BF)


def kernel(
    mass, bins, tau, mask, absb, alb, cosz, ext, ssa, asy, gas, sol, band, lr, w, b, hw,
    flux, head, tg, bg,
    tab, gcol, m0, opt, refl, trans, below, down,
    slot_col, fs, fr, fz, fx, fo, ts, tr, tz, tx, to, wz, bs, br, bz, hv, hwt, biasc,
    xs, pre, slope, ht, pp, po, gt, ta, tps, bps, tpr, bpr, fsum, fbsum, gr, gb, hg,
    s_w, r_w, s_b, r_b, s_f, r_f, s_wz, r_wz, s_bz, r_bz, s_fz, r_fz, s_fd, r_fd,
    s_t, r_t, s_tz, r_tz, s_td, r_td, s_p, r_p, s_h, r_h, l_h, l_hw,
    s_k, r_k, s_kb, r_kb, s_e, r_e, s_eb, r_eb,
):
    zh, cc, x, zl, y = (lax.axis_index(a) for a in GRP_LRN)
    other = 1 - cc
    me = x * 8 + y
    z = zh * 4 + zl
    part = 2 * cc + zh
    own_piece = (part == x) & (x == zl)

    def plane(i):
        p = lax.rem(me + i, 32)
        return p, lax.div(p, 8), lax.rem(p, 8)

    def ring(i):
        q = lax.rem(z + i, 8)
        return lax.div(q, 4), lax.rem(q, 4)

    barrier = pltpu.get_barrier_semaphore()

    def greet(i, c):
        _, px, py = plane(i)
        pl.semaphore_signal(barrier, inc=1, device_id={"x": px, "y": py}, device_id_type=MESH)
        return c

    lax.fori_loop(1, 32, greet, 0)
    for i in range(1, 8):
        qh, ql = ring(i)
        pl.semaphore_signal(barrier, inc=1, device_id={"zh": qh, "zl": ql}, device_id_type=MESH)
    pl.semaphore_signal(barrier, inc=1, device_id={"cc": other}, device_id_type=MESH)
    for a in range(4):

        @pl.when(jnp.logical_not(own_piece & (zl == a)))
        def _():
            at = {"zh": lax.rem(x, 2), "cc": lax.div(x, 2), "x": zl, "zl": a}
            pl.semaphore_signal(barrier, inc=1, device_id=at, device_id_type=MESH)

    hw_copy = pltpu.make_async_copy(hw.at[pl.ds(2 * cc, 2)], hv, l_hw)
    hw_copy.start()

    send_features(mass, bins, lr, fs, slot_col)
    spread = (iota((16, COL_DEV), 1) == y * 16 + iota((16, COL_DEV), 0)).astype(BF)
    bs[...] = nn(b[...], spread)
    sender = lax.div(x, 2) == cc
    xb = lax.rem(x, 2)

    @pl.when(own_piece)
    def _():
        pl.semaphore_wait(barrier, 42)

    @pl.when(jnp.logical_not(own_piece))
    def _():
        pl.semaphore_wait(barrier, 43)

    @pl.when(sender)
    def _():
        def go(i, c):
            _, px, py = plane(i)
            remote(w, wz.at[xb, zl, y], s_w, r_w, x=px, y=py).start()
            remote(bs, br.at[xb, y], s_b, r_b, x=px, y=py).start()
            return c

        lax.fori_loop(1, 32, go, 0)
        wz[xb, zl, y] = w[...]
        br[xb, y] = bs[...]

    def go_features(i, c):
        p, px, py = plane(i)
        remote(fs.at[p], fr.at[me], s_f, r_f, x=px, y=py).start()
        return c

    lax.fori_loop(1, 32, go_features, 0)
    fr[me] = fs[me]

    bcol = evolve_setup(ext, ssa, asy, gas, sol, band, tab, gcol, m0)
    evolve_layers(mass, bins, tau, mask, absb, tab, gcol, opt, refl, trans)

    @pl.when(sender)
    def _():
        wait_bytes(tpr.at[0:15], r_w)
        wait_bytes(bpr.at[0:15], r_b)

    @pl.when(jnp.logical_not(sender))
    def _():
        wait_bytes(tpr.at[0:16], r_w)
        wait_bytes(bpr.at[0:16], r_b)

    for a in range(2):
        bz[a, zl] = jnp.sum(br[a], axis=0)
    for step in (1, 7, 2 + 4 * cc):
        qh, ql = ring(step)
        remote(wz.at[:, zl], wz.at[:, zl], s_wz, r_wz, zh=qh, zl=ql).start()
        remote(bz.at[:, zl], bz.at[:, zl], s_bz, r_bz, zh=qh, zl=ql).start()

    wait_bytes(fr.at[0:31], r_f)
    got = fr[...].reshape(512, COL_DEV)
    o = iota((COL_DEV, 512), 0)
    source = ((o >> 1) & 31) * 16 + (o >> 6) * 2 + (o & 1)
    shift = iota((COL_DEV, 512), 1) - source
    for a in range(4):
        pick = jnp.where(shift == 4 * a, 1.0, 0.0).astype(BF)
        fz[a] = nn(pick, got).astype(BF)
    for i in (4, 3, 5, 2, 6, 1, 7):
        qh, ql = ring(i)
        remote(fz.at[ql], fx.at[z], s_fz, r_fz, zh=qh, zl=ql).start()
    fx[z] = fz[zl]

    evolve_up(alb, bcol, refl, trans, below)
    evolve_down(sol, cosz, m0, below, trans, down, flux)

    place = jnp.where(iota((256, COL_DEV), 0) == slot_col[...], 1.0, 0.0).astype(BF)
    ts[...] = nt(place, flux[...].astype(BF)).reshape(32, 8, COL_DEV).astype(BF)

    def go_targets(i, c):
        p, px, py = plane(i)
        remote(ts.at[p], tr.at[me], s_t, r_t, x=px, y=py).start()
        return c

    lax.fori_loop(1, 32, go_targets, 0)
    tr[me] = ts[me]

    hw_copy.wait()
    eye = jnp.where(iota((COL_DEV, COL_DEV), 0) == iota((COL_DEV, COL_DEV), 1), 1.0, 0.0).astype(BF)
    for a in range(2):
        hwt[a] = nt(eye, hv[a]).astype(BF)
    wait_bytes(fx.at[0:7], r_fz)
    fd = remote(fx, fo, s_fd, r_fd, cc=other)
    fd.start()
    wait_bytes(bz.at[:, 0:3], r_bz)
    for a in range(2):
        for q in range(4):
            biasc[a, q * COL_DEV : (q + 1) * COL_DEV, :] = jnp.broadcast_to(row_to_col(bz[a, q]), (COL_DEV, COL_DEV))
    wait_bytes(wz.at[:, 0:3], r_wz)

    def gather_x(side, ref):
        for q in range(8):
            for h in range(2):
                xs[side * 2 + q // 4, (q % 4) * 64 : (q % 4 + 1) * 64, h * COL_DEV : (h + 1) * COL_DEV] = ref[
                    q, h * 64 : (h + 1) * 64, :
                ]

    gather_x(0, fx)

    def forward(sb, half, with_slope):
        pre[...] = nt(wz[half].reshape(512, 256), xs[sb])
        for r in range(0, 512, 32):
            v = pre[r : r + 32, :]
            bc = biasc[half, r : r + 32, :]
            v = v + jnp.concatenate([bc, bc], axis=1)
            sq = v * v
            t = jnp.tanh(ROOT * (v + CUBE * (v * sq)))
            cdf = 0.5 + 0.5 * t
            ht[sb, half, r : r + 32, :] = (v * cdf).astype(BF)
            if with_slope:
                slope[sb, r : r + 32, :] = cdf + (0.5 * v) * ((1.0 - t * t) * (ROOT + (3.0 * CUBE * ROOT) * sq))
        return nn(hwt[half], ht[sb, half])

    def forward_block(sb, c):
        pp[sb] = forward(sb, zh, True) + forward(sb, 1 - zh, False)
        return c

    lax.fori_loop(0, 2, forward_block, 0)

    wait_bytes(tr.at[0:31], r_t)
    gott = tr[...].astype(F32).reshape(256, COL_DEV).astype(BF)
    ot = iota((64, 256), 0)
    shift_t = iota((64, 256), 1) - ((ot >> 1) * 8 + (ot & 1))
    for a in range(4):
        tz[a] = nn(jnp.where(shift_t == 2 * a, 1.0, 0.0).astype(BF), gott).astype(BF)
    for i in (4, 3, 5, 2, 6, 1, 7):
        qh, ql = ring(i)
        remote(tz.at[ql], tx.at[z], s_tz, r_tz, zh=qh, zl=ql).start()
    tx[z] = tz[zl]

    fd.wait()
    gather_x(1, fo)
    lax.fori_loop(2, 4, forward_block, 0)
    pd = remote(pp, po, s_p, r_p, cc=other)
    pd.start()

    wait_bytes(tx.at[0:7], r_tz)
    td = remote(tx, to, s_td, r_td, cc=other)
    td.start()
    pd.wait()
    td.wait()
    lane0 = jnp.where(iota((8, COL_DEV), 1) == 0, 1.0, 0.0).astype(BF)
    for sb in range(4):
        src = (tx, tx, to, to)[sb]
        goal = nt(eye, src[(sb % 2) * 4 : (sb % 2) * 4 + 4].reshape(256, COL_DEV))
        flag = nt(lane0, xs[sb, :, COL_DEV:])[0:1, :]
        factor = jnp.where(flag < 1.5, 1.0 / COL_DEV, 0.0)
        gt[sb] = (((pp[sb] + po[(sb + 2) % 4]) - goal) * factor).astype(BF)

    ones = jnp.ones((8, 256), BF)
    ta[...] = jnp.zeros_like(ta)

    def backward(sb, brow):
        hgrad = nn(hv[zh], gt[sb])
        pgrad = (hgrad * slope[sb]).astype(BF)
        ta[...] += nn(pgrad, xs[sb])
        return brow + nt(ones, pgrad)

    brow = lax.fori_loop(0, 4, backward, jnp.zeros((8, 512), F32))
    tps[...] = ta[...].reshape(32, 16, 256).astype(BF)
    for a in range(4):
        bps[a] = brow[0:1, a * COL_DEV : (a + 1) * COL_DEV]

    def go_trunk(i, c):
        p, px, py = plane(i)
        remote(tps.at[p], tpr.at[me], s_k, r_k, x=px, y=py).start()
        remote(bps.at[px], bpr.at[me], s_kb, r_kb, x=px, y=py).start()
        return c

    lax.fori_loop(1, 32, go_trunk, 0)
    tpr[me] = tps[me]
    bpr[me] = bps[x]

    for half in range(2):
        total = nt(ht[0, half], gt[0])
        for sb in range(1, 4):
            total = total + nt(ht[sb, half], gt[sb])
        hg[half] = total
    hd = remote(hg, head.at[pl.ds(2 * cc, 2)], s_h, r_h, cc=other)
    hd.start()
    hl = pltpu.make_async_copy(hg, head.at[pl.ds(2 * cc, 2)], l_h)
    hl.start()

    wait_bytes(tpr.at[0:31], r_k)
    wait_bytes(bpr.at[0:31], r_kb)
    fsum[...] = jnp.sum(tpr[...].astype(F32), axis=0)
    fbsum[...] = jnp.sum(bpr[...], axis=0)
    for qh in range(2):
        for qc in range(2):
            mine = own_piece & (zh == qh) & (cc == qc)

            @pl.when(jnp.logical_not(mine))
            def _():
                at = dict(zh=qh, cc=qc, x=part, zl=x)
                remote(fsum, gr.at[zl], s_e, r_e, **at).start()
                remote(fbsum, gb.at[zl], s_eb, r_eb, **at).start()

            @pl.when(mine)
            def _():
                gr[zl] = fsum[...]
                gb[zl] = fbsum[...]

    @pl.when(own_piece)
    def _():
        wait_bytes(gr.at[0:3], r_e)
        wait_bytes(gb.at[0:3], r_eb)

    @pl.when(jnp.logical_not(own_piece))
    def _():
        wait_bytes(gr, r_e)
        wait_bytes(gb, r_eb)

    tg[...] = (gr[0] + gr[1]) + (gr[2] + gr[3])
    brows = (gb[0] + gb[1]) + (gb[2] + gb[3])
    kept = jnp.where(lax.div(iota((1, COL_DEV), 1), 16) == y, brows, 0.0)
    bias = kept[:, 0:16]
    for a in range(1, 8):
        bias = bias + kept[:, a * 16 : (a + 1) * 16]
    bg[...] = bias

    hl.wait()
    hd.wait_send()
    wait_bytes(head.at[pl.ds(2 * other, 2)], r_h)

    @pl.when(sender)
    def _():
        wait_bytes(tpr.at[0:31], s_w)
        wait_bytes(bpr.at[0:31], s_b)

    wait_bytes(fs.at[0:31], s_f)
    wait_bytes(wz.at[:, 0:3], s_wz)
    wait_bytes(bz.at[:, 0:3], s_bz)
    wait_bytes(fx.at[0:7], s_fz)
    wait_bytes(ts.at[0:31], s_t)
    wait_bytes(tx.at[0:7], s_tz)
    wait_bytes(tps.at[0:31], s_k)
    wait_bytes(bpr.at[0:31], s_kb)

    @pl.when(own_piece)
    def _():
        wait_bytes(gr.at[0:3], s_e)
        wait_bytes(gb.at[0:3], s_eb)

    @pl.when(jnp.logical_not(own_piece))
    def _():
        wait_bytes(gr, s_e)
        wait_bytes(gb, s_eb)


def per_device(mass, bins, tau, mask, absb, alb, cosz, ext, ssa, asy, gas, sol, band, lr, w, b, hw):
    vm = pl.BlockSpec(memory_space=pltpu.VMEM)
    hbm = pl.BlockSpec(memory_space=pl.ANY)
    v = pltpu.VMEM
    c = COL_DEV
    flux, head, tg, bg = pl.pallas_call(
        kernel,
        out_shape=(
            jax.ShapeDtypeStruct((4 * LEV, c), F32),
            jax.ShapeDtypeStruct((4, 512, c), F32),
            jax.ShapeDtypeStruct((16, 256), F32),
            jax.ShapeDtypeStruct((1, 16), F32),
        ),
        in_specs=[vm] * 16 + [hbm],
        out_specs=(vm, hbm, vm, vm),
        scratch_shapes=[
            v((3 * G, MODES * BINS), BF), v((G, c), F32), v((G, c), F32), v((3 * G, LU * c), F32),
            v((LEV, G, c), F32), v((LEV, G, c), F32), v((LEV + 1, G, c), F32), v((G, c), F32),
            v((1, c), jnp.int32),
            v((32, 16, c), BF), v((32, 16, c), BF), v((4, 128, c), BF), v((8, 128, c), BF), v((8, 128, c), BF),
            v((32, 8, c), BF), v((32, 8, c), BF), v((4, 64, c), BF), v((8, 64, c), BF), v((8, 64, c), BF),
            v((2, 4, 8, 16, 256), BF), v((1, c), F32), v((2, 8, 1, c), F32), v((2, 4, 1, c), F32),
            v((2, 512, c), BF), v((2, c, 512), BF), v((2, 512, c), F32),
            v((4, 256, 256), BF), v((512, 256), F32), v((4, 512, 256), F32), v((4, 2, 512, 256), BF),
            v((4, c, 256), F32), v((4, c, 256), F32), v((4, c, 256), BF), v((512, 256), F32),
            v((32, 16, 256), BF), v((4, 1, c), F32), v((32, 16, 256), BF), v((32, 1, c), F32),
            v((16, 256), F32), v((1, c), F32), v((4, 16, 256), F32), v((4, 1, c), F32), v((2, 512, c), F32),
        ] + [pltpu.SemaphoreType.DMA] * 34,
        compiler_params=pltpu.CompilerParams(collective_id=0, has_side_effects=True),
    )(
        mass, bins, tau, mask[None], absb, alb, cosz[None], ext, ssa, asy, gas[None], sol[None], band[None],
        lr.reshape(1, c), w, b[None], hw.reshape(4, 512, c),
    )
    return flux, head.reshape(1, 2048, c), tg, bg[0]


def solution(mesh):
    split = Mesh(mesh.devices.reshape(2, 2, 4, 4, 8), GRP_LRN)
    placed = (
        P(None, None, GRP_LRN),
        P(None, None, GRP_LRN),
        P(None, GRP_LRN),
        P(GRP_LRN),
        P(None, GRP_LRN),
        P(None, GRP_LRN),
        P(GRP_LRN),
        P(),
        P(),
        P(),
        P(),
        P(),
        P(),
        P(GRP_LRN, None),
        P(LRN, None),
        P(LRN),
        P(LRN, None, None),
    )
    return jax.shard_map(
        per_device,
        mesh=split,
        in_specs=placed,
        out_specs=(P(None, GRP_LRN), P(LRN, None, None), P(LRN, None), P(LRN)),
        check_vma=False,
    )
```

time: 247 us -> 70.3 us (0.28)
  the two profiles are of different devices: /device:TPU:64 before, /device:TPU:3 now
where the time goes in v2:
time: 70.3 us; the launch traced here: 70.1 us
  Pallas kernels  64.5 us (92%)
  local copies, waits for them, and re-layouts  4.93 us (7%)
    pallas_call x1, Pallas kernels, per_device(): pl.pallas_call(kernel, out_shape=(jax.ShapeDtypeStruct((4 * LEV, c), F32)...  64.5 us
    unnamed x8, local copies, waits for them, and re-layouts  4.93 us

profile of v2, /device:TPU:3, one launch (start us, length us, event | category | flops | bytes accessed | tf_op | source)
XLA Modules:
  0.0 70.1 jit_solution(2800534847918434532)
XLA Ops:
  0.6 64.5 %shard_map.192 = (f32[128,128]{1,0:T(8,128)}, f32[4,512,128]{2,1,0:T(8,128)}, f32[16,256]{1,0:T(8,128)}, f32[1,16]{1,0:T(1,128)}) custom-call(f32[4,32,128]{2,1,0:T(8,128)} %mass.1, s32[4,32,128]{2,1,0:T(8,128)} %bins.1, f32[32,128]{1,0:T(8,128)} %tau.1, s32[1,128]{1,0:T(1,128)} %bitcast.12, f32[32,128]{1,0:T(8,128)} %absb.1, f32[14,128]{1,0:T(8,128)} %alb.1, ...), custom_call_target="tpu_custom_call" | custom-call | tf_op jit(solution)/shard_map/pallas_call | solution.py:490
  65.2 1.5 %copy.25 = f32[128,128]{1,0:T(8,128)} copy(f32[128,128]{1,0:T(8,128)} %get-tuple-element.16) | data formatting | bytes 131072
  66.7 0.0 copy-start
  66.7 2.3 %copy.26 = f32[1,2048,128]{2,1,0:T(8,128)} copy(f32[1,2048,128]{2,1,0:T(8,128)} %bitcast.10) | data formatting | bytes 2097152
  68.9 0.0 copy-done
  68.9 0.0 copy-start.1
  68.9 0.6 copy.27
  69.6 0.1 copy-done.1
  69.6 0.5 copy.28
Async XLA Ops:
  66.7 2.3 %copy-start = (f32[16,256]{1,0:T(8,128)S(1)}, f32[16,256]{1,0:T(8,128)}, u32[]{:S(2)}) copy-start(f32[16,256]{1,0:T(8,128)} %get-tuple-element.18) | copy-start | bytes 49156
  68.9 0.7 copy-start.1

commit v3 on v2

--- a/solution.py
+++ b/solution.py
@@ -106,17 +106,18 @@
 
     def body(step, carry):
         l = LEV - 1 - step
-        for g in range(0, G, CH):
-            rows = slice(g, g + CH)
-            b = below[l + 1, rows, :]
-            r = refl[l, rows, :]
-            t = trans[l, rows, :]
+        layer = [(refl[l, g : g + CH, :], trans[l, g : g + CH, :]) for g in range(0, G, CH)]
+        nxt, ratio = [], []
+        for b, (r, t) in zip(carry, layer):
             q = t / (1.0 - r * b)
-            below[l, rows, :] = r + t * b * q
-            trans[l, rows, :] = q
-        return carry
-
-    lax.fori_loop(0, LEV, body, 0)
+            ratio.append(q)
+            nxt.append(r + t * b * q)
+        for i, g in enumerate(range(0, G, CH)):
+            below[l, g : g + CH, :] = nxt[i]
+            trans[l, g : g + CH, :] = ratio[i]
+        return tuple(nxt)
+
+    lax.fori_loop(0, LEV, body, tuple(surface[g : g + CH, :] for g in range(0, G, CH)))
 
 
 def evolve_down(sol, cosz, m0, below, trans, down, flux):
@@ -183,13 +184,15 @@
 
 
 def kernel(
-    mass, bins, tau, mask, absb, alb, cosz, ext, ssa, asy, gas, sol, band, lr, w, b, hw,
+    mass_in, bins_in, tau_in, mask_in, absb_in, alb_in, cosz_in, ext_in, ssa_in, asy_in, gas_in, sol_in, band_in,
+    lr_in, w_in, b_in, hw,
     flux, head, tg, bg,
+    mass, bins, tau, mask, absb, alb, cosz, ext, ssa, asy, gas, sol, band, lr, w, b, in_sems,
     tab, gcol, m0, opt, refl, trans, below, down,
-    slot_col, fs, fr, fz, fx, fo, ts, tr, tz, tx, to, wz, bs, br, bz, hv, hwt, biasc,
+    slot_col, fs, fr, fz, fx, fo, ts, tr, tz, tx, to, wa, wb, wl, bs, br, bz, hv, hwt, biasc,
     xs, pre, slope, ht, pp, po, gt, ta, tps, bps, tpr, bpr, fsum, fbsum, gr, gb, hg,
-    s_w, r_w, s_b, r_b, s_f, r_f, s_wz, r_wz, s_bz, r_bz, s_fz, r_fz, s_fd, r_fd,
-    s_t, r_t, s_tz, r_tz, s_td, r_td, s_p, r_p, s_h, r_h, l_h, l_hw,
+    s_w, r_w, s_b, r_b, s_f, r_f, s_wz, r_wz, s_bz, r_bz, s_wl, r_wl, s_wy, r_wy, s_wx, r_wx, s_fz, r_fz, s_fd, r_fd,
+    s_t, r_t, s_tz, r_tz, s_td, r_td, s_p, r_p, s_p1, r_p1, s_h, r_h, l_h, l_hw,
     s_k, r_k, s_kb, r_kb, s_e, r_e, s_eb, r_eb,
 ):
     zh, cc, x, zl, y = (lax.axis_index(a) for a in GRP_LRN)
@@ -207,14 +210,17 @@
         q = lax.rem(z + i, 8)
         return lax.div(q, 4), lax.rem(q, 4)
 
+    pairs = [
+        (lr_in, lr), (mass_in, mass), (bins_in, bins), (w_in, w), (b_in, b), (ext_in, ext), (ssa_in, ssa),
+        (asy_in, asy), (gas_in, gas), (band_in, band), (tau_in, tau), (mask_in, mask), (absb_in, absb),
+        (alb_in, alb), (cosz_in, cosz), (sol_in, sol),
+    ]
+    loads = [pltpu.make_async_copy(src, dst, in_sems.at[i]) for i, (src, dst) in enumerate(pairs)]
     barrier = pltpu.get_barrier_semaphore()
 
-    def greet(i, c):
+    for i in range(1, 32):
         _, px, py = plane(i)
         pl.semaphore_signal(barrier, inc=1, device_id={"x": px, "y": py}, device_id_type=MESH)
-        return c
-
-    lax.fori_loop(1, 32, greet, 0)
     for i in range(1, 8):
         qh, ql = ring(i)
         pl.semaphore_signal(barrier, inc=1, device_id={"zh": qh, "zl": ql}, device_id_type=MESH)
@@ -226,9 +232,13 @@
             at = {"zh": lax.rem(x, 2), "cc": lax.div(x, 2), "x": zl, "zl": a}
             pl.semaphore_signal(barrier, inc=1, device_id=at, device_id_type=MESH)
 
+    for load in loads:
+        load.start()
     hw_copy = pltpu.make_async_copy(hw.at[pl.ds(2 * cc, 2)], hv, l_hw)
     hw_copy.start()
 
+    for load in loads[:5]:
+        load.wait()
     send_features(mass, bins, lr, fs, slot_col)
     spread = (iota((16, COL_DEV), 1) == y * 16 + iota((16, COL_DEV), 0)).astype(BF)
     bs[...] = nn(b[...], spread)
@@ -243,17 +253,14 @@
     def _():
         pl.semaphore_wait(barrier, 43)
 
+    z_steps = (1, 7, 2 + 4 * cc)
+
     @pl.when(sender)
     def _():
-        def go(i, c):
-            _, px, py = plane(i)
-            remote(w, wz.at[xb, zl, y], s_w, r_w, x=px, y=py).start()
-            remote(bs, br.at[xb, y], s_b, r_b, x=px, y=py).start()
-            return c
-
-        lax.fori_loop(1, 32, go, 0)
-        wz[xb, zl, y] = w[...]
-        br[xb, y] = bs[...]
+        for i in z_steps:
+            qh, ql = ring(i)
+            remote(w.at[:, COL_DEV:], wl.at[zl], s_wl, r_wl, zh=qh, zl=ql).start()
+        wl[zl] = w[:, COL_DEV:]
 
     def go_features(i, c):
         p, px, py = plane(i)
@@ -263,25 +270,29 @@
     lax.fori_loop(1, 32, go_features, 0)
     fr[me] = fs[me]
 
+    @pl.when(sender)
+    def _():
+        def go(i, c):
+            _, px, py = plane(i)
+            remote(w.at[:, 0:COL_DEV], wa.at[xb, zl, y], s_w, r_w, x=px, y=py).start()
+            remote(bs, br.at[xb, y], s_b, r_b, x=px, y=py).start()
+            return c
+
+        lax.fori_loop(1, 32, go, 0)
+        wa[xb, zl, y] = w[:, 0:COL_DEV]
+        br[xb, y] = bs[...]
+
+    for load in loads[5:]:
+        load.wait()
     bcol = evolve_setup(ext, ssa, asy, gas, sol, band, tab, gcol, m0)
     evolve_layers(mass, bins, tau, mask, absb, tab, gcol, opt, refl, trans)
 
     @pl.when(sender)
     def _():
-        wait_bytes(tpr.at[0:15], r_w)
-        wait_bytes(bpr.at[0:15], r_b)
-
-    @pl.when(jnp.logical_not(sender))
-    def _():
-        wait_bytes(tpr.at[0:16], r_w)
-        wait_bytes(bpr.at[0:16], r_b)
-
-    for a in range(2):
-        bz[a, zl] = jnp.sum(br[a], axis=0)
-    for step in (1, 7, 2 + 4 * cc):
-        qh, ql = ring(step)
-        remote(wz.at[:, zl], wz.at[:, zl], s_wz, r_wz, zh=qh, zl=ql).start()
-        remote(bz.at[:, zl], bz.at[:, zl], s_bz, r_bz, zh=qh, zl=ql).start()
+        wait_bytes(fr.at[0:3], r_wl)
+        for i in range(1, 8):
+            remote(wl, wb.at[xb, :, y], s_wy, r_wy, y=lax.rem(y + i, 8)).start()
+        wb[xb, :, y] = wl[...]
 
     wait_bytes(fr.at[0:31], r_f)
     got = fr[...].reshape(512, COL_DEV)
@@ -310,48 +321,33 @@
     lax.fori_loop(1, 32, go_targets, 0)
     tr[me] = ts[me]
 
+    @pl.when(sender)
+    def _():
+        wait_bytes(fr.at[0:15], r_w)
+        wait_bytes(bpr.at[0:15], r_b)
+
+    @pl.when(jnp.logical_not(sender))
+    def _():
+        wait_bytes(fr.at[0:16], r_w)
+        wait_bytes(bpr.at[0:16], r_b)
+
+    for a in range(2):
+        bz[a, zl] = jnp.sum(br[a], axis=0)
+    for i in z_steps:
+        qh, ql = ring(i)
+        remote(wa.at[:, zl], wa.at[:, zl], s_wz, r_wz, zh=qh, zl=ql).start()
+        remote(bz.at[:, zl], bz.at[:, zl], s_bz, r_bz, zh=qh, zl=ql).start()
+
+    @pl.when(sender)
+    def _():
+        wait_bytes(fr.at[0:28], r_wy)
+        for i in (1, 3, 2):
+            remote(wb.at[xb], wb.at[xb], s_wx, r_wx, x=lax.rem(x + i, 4)).start()
+
     hw_copy.wait()
     eye = jnp.where(iota((COL_DEV, COL_DEV), 0) == iota((COL_DEV, COL_DEV), 1), 1.0, 0.0).astype(BF)
     for a in range(2):
         hwt[a] = nt(eye, hv[a]).astype(BF)
-    wait_bytes(fx.at[0:7], r_fz)
-    fd = remote(fx, fo, s_fd, r_fd, cc=other)
-    fd.start()
-    wait_bytes(bz.at[:, 0:3], r_bz)
-    for a in range(2):
-        for q in range(4):
-            biasc[a, q * COL_DEV : (q + 1) * COL_DEV, :] = jnp.broadcast_to(row_to_col(bz[a, q]), (COL_DEV, COL_DEV))
-    wait_bytes(wz.at[:, 0:3], r_wz)
-
-    def gather_x(side, ref):
-        for q in range(8):
-            for h in range(2):
-                xs[side * 2 + q // 4, (q % 4) * 64 : (q % 4 + 1) * 64, h * COL_DEV : (h + 1) * COL_DEV] = ref[
-                    q, h * 64 : (h + 1) * 64, :
-                ]
-
-    gather_x(0, fx)
-
-    def forward(sb, half, with_slope):
-        pre[...] = nt(wz[half].reshape(512, 256), xs[sb])
-        for r in range(0, 512, 32):
-            v = pre[r : r + 32, :]
-            bc = biasc[half, r : r + 32, :]
-            v = v + jnp.concatenate([bc, bc], axis=1)
-            sq = v * v
-            t = jnp.tanh(ROOT * (v + CUBE * (v * sq)))
-            cdf = 0.5 + 0.5 * t
-            ht[sb, half, r : r + 32, :] = (v * cdf).astype(BF)
-            if with_slope:
-                slope[sb, r : r + 32, :] = cdf + (0.5 * v) * ((1.0 - t * t) * (ROOT + (3.0 * CUBE * ROOT) * sq))
-        return nn(hwt[half], ht[sb, half])
-
-    def forward_block(sb, c):
-        pp[sb] = forward(sb, zh, True) + forward(sb, 1 - zh, False)
-        return c
-
-    lax.fori_loop(0, 2, forward_block, 0)
-
     wait_bytes(tr.at[0:31], r_t)
     gott = tr[...].astype(F32).reshape(256, COL_DEV).astype(BF)
     ot = iota((64, 256), 0)
@@ -363,16 +359,65 @@
         remote(tz.at[ql], tx.at[z], s_tz, r_tz, zh=qh, zl=ql).start()
     tx[z] = tz[zl]
 
+    wait_bytes(fx.at[0:7], r_fz)
+    fd = remote(fx, fo, s_fd, r_fd, cc=other)
+    fd.start()
+    wait_bytes(bz.at[:, 0:3], r_bz)
+    for a in range(2):
+        for q in range(4):
+            biasc[a, q * COL_DEV : (q + 1) * COL_DEV, :] = jnp.broadcast_to(row_to_col(bz[a, q]), (COL_DEV, COL_DEV))
+    wait_bytes(wa.at[:, 0:3], r_wz)
+
+    @pl.when(sender)
+    def _():
+        wait_bytes(wb.at[0], r_wx)
+
+    @pl.when(jnp.logical_not(sender))
+    def _():
+        wait_bytes(wb, r_wx)
+
+    def gather_x(side, ref):
+        for q in range(8):
+            for h in range(2):
+                xs[side * 2 + q // 4, (q % 4) * 64 : (q % 4 + 1) * 64, h * COL_DEV : (h + 1) * COL_DEV] = ref[
+                    q, h * 64 : (h + 1) * 64, :
+                ]
+
+    gather_x(0, fx)
+
+    def forward(sb, half, with_slope):
+        rows = jnp.concatenate([wa[half].reshape(512, COL_DEV), wb[half].reshape(512, COL_DEV)], axis=1)
+        pre[...] = nt(rows, xs[sb])
+        for r in range(0, 512, 32):
+            v = pre[r : r + 32, :]
+            bc = biasc[half, r : r + 32, :]
+            v = v + jnp.concatenate([bc, bc], axis=1)
+            sq = v * v
+            t = jnp.tanh(v * (ROOT + (ROOT * CUBE) * sq))
+            cdf = 0.5 + 0.5 * t
+            ht[sb, half, r : r + 32, :] = (v * cdf).astype(BF)
+            if with_slope:
+                slope[sb, r : r + 32, :] = cdf + (0.5 * v) * ((1.0 - t * t) * (ROOT + (3.0 * CUBE * ROOT) * sq))
+        return nn(hwt[half], ht[sb, half])
+
+    def forward_block(sb, c):
+        pp[sb] = forward(sb, zh, True) + forward(sb, 1 - zh, False)
+        return c
+
+    lax.fori_loop(0, 2, forward_block, 0)
+    pd = remote(pp.at[0:2], po.at[0:2], s_p, r_p, cc=other)
+    pd.start()
     fd.wait()
     gather_x(1, fo)
     lax.fori_loop(2, 4, forward_block, 0)
-    pd = remote(pp, po, s_p, r_p, cc=other)
-    pd.start()
+    pd1 = remote(pp.at[2:4], po.at[2:4], s_p1, r_p1, cc=other)
+    pd1.start()
 
     wait_bytes(tx.at[0:7], r_tz)
     td = remote(tx, to, s_td, r_td, cc=other)
     td.start()
     pd.wait()
+    pd1.wait()
     td.wait()
     lane0 = jnp.where(iota((8, COL_DEV), 1) == 0, 1.0, 0.0).astype(BF)
     for sb in range(4):
@@ -383,26 +428,31 @@
         gt[sb] = (((pp[sb] + po[(sb + 2) % 4]) - goal) * factor).astype(BF)
 
     ones = jnp.ones((8, 256), BF)
-    ta[...] = jnp.zeros_like(ta)
-
-    def backward(sb, brow):
-        hgrad = nn(hv[zh], gt[sb])
-        pgrad = (hgrad * slope[sb]).astype(BF)
-        ta[...] += nn(pgrad, xs[sb])
-        return brow + nt(ones, pgrad)
-
-    brow = lax.fori_loop(0, 4, backward, jnp.zeros((8, 512), F32))
-    tps[...] = ta[...].reshape(32, 16, 256).astype(BF)
-    for a in range(4):
-        bps[a] = brow[0:1, a * COL_DEV : (a + 1) * COL_DEV]
-
-    def go_trunk(i, c):
-        p, px, py = plane(i)
-        remote(tps.at[p], tpr.at[me], s_k, r_k, x=px, y=py).start()
-        remote(bps.at[px], bpr.at[me], s_kb, r_kb, x=px, y=py).start()
-        return c
-
-    lax.fori_loop(1, 32, go_trunk, 0)
+    for part_of in range(2):
+        units = slice(part_of * 256, part_of * 256 + 256)
+        brow = jnp.zeros((8, 256), F32)
+        for sb in range(4):
+            hgrad = nn(hv[zh, units, :], gt[sb])
+            pgrad = (hgrad * slope[sb, units, :]).astype(BF)
+            term = nn(pgrad, xs[sb])
+            ta[...] = term if sb == 0 else ta[...] + term
+            brow = brow + nt(ones, pgrad)
+        tps[part_of * 16 : part_of * 16 + 16] = ta[...].reshape(16, 16, 256).astype(BF)
+        for a in range(2):
+            bps[part_of * 2 + a] = brow[0:1, a * COL_DEV : (a + 1) * COL_DEV]
+
+        def go_trunk(i, c, part_of=part_of):
+            p = part_of * 16 + lax.rem(me + i, 16)
+            px, py = lax.div(p, 8), lax.rem(p, 8)
+
+            @pl.when(p != me)
+            def _():
+                remote(tps.at[p], tpr.at[me], s_k, r_k, x=px, y=py).start()
+                remote(bps.at[px], bpr.at[me], s_kb, r_kb, x=px, y=py).start()
+
+            return c
+
+        lax.fori_loop(0, 16, go_trunk, 0)
     tpr[me] = tps[me]
     bpr[me] = bps[x]
 
@@ -459,11 +509,14 @@
 
     @pl.when(sender)
     def _():
-        wait_bytes(tpr.at[0:31], s_w)
+        wait_bytes(fr.at[0:31], s_w)
         wait_bytes(bpr.at[0:31], s_b)
+        wait_bytes(fr.at[0:3], s_wl)
+        wait_bytes(fr.at[0:28], s_wy)
+        wait_bytes(xs.at[0:3], s_wx)
 
     wait_bytes(fs.at[0:31], s_f)
-    wait_bytes(wz.at[:, 0:3], s_wz)
+    wait_bytes(wa.at[:, 0:3], s_wz)
     wait_bytes(bz.at[:, 0:3], s_bz)
     wait_bytes(fx.at[0:7], s_fz)
     wait_bytes(ts.at[0:31], s_t)
@@ -480,6 +533,20 @@
     def _():
         wait_bytes(gr, s_e)
         wait_bytes(gb, s_eb)
+
+
+def copy_out(flux_in, head_in, tg_in, bg_in, flux, head, tg, bg, vflux, vhead, vtg, vbg, sems):
+    trips = [(head_in.at[i], vhead.at[i], head.at[i]) for i in range(4)]
+    trips += [(flux_in, vflux, flux), (tg_in, vtg, tg), (bg_in, vbg, bg)]
+    ins = [pltpu.make_async_copy(a, b, sems.at[0, i]) for i, (a, b, _) in enumerate(trips)]
+    outs = [pltpu.make_async_copy(b, c, sems.at[1, i]) for i, (_, b, c) in enumerate(trips)]
+    for copy in ins:
+        copy.start()
+    for copy, out in zip(ins, outs):
+        copy.wait()
+        out.start()
+    for out in outs:
+        out.wait()
 
 
 def per_device(mass, bins, tau, mask, absb, alb, cosz, ext, ssa, asy, gas, sol, band, lr, w, b, hw):
@@ -495,26 +562,37 @@
             jax.ShapeDtypeStruct((16, 256), F32),
             jax.ShapeDtypeStruct((1, 16), F32),
         ),
-        in_specs=[vm] * 16 + [hbm],
+        in_specs=[hbm] * 17,
         out_specs=(vm, hbm, vm, vm),
         scratch_shapes=[
+            v((MODES, LEV, c), F32), v((MODES, LEV, c), jnp.int32), v((LEV, c), F32), v((1, c), jnp.int32),
+            v((LEV, c), F32), v((NB, c), F32), v((1, c), F32), v((G, 256), F32), v((G, 256), F32), v((G, 256), F32),
+            v((1, G), F32), v((1, G), F32), v((1, G), jnp.int32), v((1, c), jnp.int32), v((16, 256), BF), v((1, 16), BF),
+            pltpu.SemaphoreType.DMA((16,)),
             v((3 * G, MODES * BINS), BF), v((G, c), F32), v((G, c), F32), v((3 * G, LU * c), F32),
             v((LEV, G, c), F32), v((LEV, G, c), F32), v((LEV + 1, G, c), F32), v((G, c), F32),
             v((1, c), jnp.int32),
             v((32, 16, c), BF), v((32, 16, c), BF), v((4, 128, c), BF), v((8, 128, c), BF), v((8, 128, c), BF),
             v((32, 8, c), BF), v((32, 8, c), BF), v((4, 64, c), BF), v((8, 64, c), BF), v((8, 64, c), BF),
-            v((2, 4, 8, 16, 256), BF), v((1, c), F32), v((2, 8, 1, c), F32), v((2, 4, 1, c), F32),
+            v((2, 4, 8, 16, c), BF), v((2, 4, 8, 16, c), BF), v((4, 16, c), BF), v((1, c), F32), v((2, 8, 1, c), F32), v((2, 4, 1, c), F32),
             v((2, 512, c), BF), v((2, c, 512), BF), v((2, 512, c), F32),
             v((4, 256, 256), BF), v((512, 256), F32), v((4, 512, 256), F32), v((4, 2, 512, 256), BF),
-            v((4, c, 256), F32), v((4, c, 256), F32), v((4, c, 256), BF), v((512, 256), F32),
+            v((4, c, 256), F32), v((4, c, 256), F32), v((4, c, 256), BF), v((256, 256), F32),
             v((32, 16, 256), BF), v((4, 1, c), F32), v((32, 16, 256), BF), v((32, 1, c), F32),
             v((16, 256), F32), v((1, c), F32), v((4, 16, 256), F32), v((4, 1, c), F32), v((2, 512, c), F32),
-        ] + [pltpu.SemaphoreType.DMA] * 34,
+        ] + [pltpu.SemaphoreType.DMA] * 42,
         compiler_params=pltpu.CompilerParams(collective_id=0, has_side_effects=True),
     )(
         mass, bins, tau, mask[None], absb, alb, cosz[None], ext, ssa, asy, gas[None], sol[None], band[None],
         lr.reshape(1, c), w, b[None], hw.reshape(4, 512, c),
     )
+    flux, head, tg, bg = pl.pallas_call(
+        copy_out,
+        out_shape=tuple(jax.ShapeDtypeStruct(a.shape, F32) for a in (flux, head, tg, bg)),
+        in_specs=[hbm] * 4,
+        out_specs=(hbm,) * 4,
+        scratch_shapes=[v(a.shape, F32) for a in (flux, head, tg, bg)] + [pltpu.SemaphoreType.DMA((2, 7))],
+    )(flux, head, tg, bg)
     return flux, head.reshape(1, 2048, c), tg, bg[0]
 
 

time: 70.3 us -> 58.8 us (0.84)
  the two profiles are of different devices: /device:TPU:3 before, /device:TPU:129 now
where the time goes in v3:
time: 58.8 us; the launch traced here: 58.6 us
  Pallas kernels  58 us (99%)
  between operations  0.65 us (1%)
    pallas_call x1, Pallas kernels, per_device(): pl.pallas_call(kernel, out_shape=(jax.ShapeDtypeStruct((4 * LEV, c), F32)...  55.9 us
    pallas_call x1, Pallas kernels, per_device(): pl.pallas_call(copy_out, out_shape=tuple((jax.ShapeDtypeStruct(a.shape, F...  2.05 us

profile of v3, /device:TPU:129, one launch (start us, length us, event | category | flops | bytes accessed | tf_op | source)
XLA Modules:
  0.0 58.6 jit_solution(9294175375247856498)
XLA Ops:
  0.6 55.9 %shard_map.192 = (f32[128,128]{1,0:T(8,128)}, f32[4,512,128]{2,1,0:T(8,128)}, f32[16,256]{1,0:T(8,128)}, f32[1,16]{1,0:T(1,128)}) custom-call(f32[4,32,128]{2,1,0:T(8,128)} %mass_in.1, s32[4,32,128]{2,1,0:T(8,128)} %bins_in.1, f32[32,128]{1,0:T(8,128)} %tau_in.1, s32[1,128]{1,0:T(1,128)} %bitcast.11, f32[32,128]{1,0:T(8,128)} %absb_in.1, f32[14,128]{1,0:T(8,128)} %alb_in.1, ...), custom_call_target="tpu_custom_call" | custom-call | tf_op jit(solution)/shard_map/pallas_call | solution.py:557
  56.6 2.1 %shard_map.193 = (f32[128,128]{1,0:T(8,128)}, f32[4,512,128]{2,1,0:T(8,128)}, f32[16,256]{1,0:T(8,128)}, f32[1,16]{1,0:T(1,128)}) custom-call(f32[128,128]{1,0:T(8,128)} %get-tuple-element.12.flux_in, f32[4,512,128]{2,1,0:T(8,128)} %get-tuple-element.13.head_in, f32[16,256]{1,0:T(8,128)} %get-tuple-element.14.tg_in, f32[1,16]{1,0:T(1,128)} %get-tuple-element.15.bg_in), custom_call_target="tpu_custom_call" | custom-call | tf_op jit(solution)/shard_map/pallas_call | solution.py:589

commit v4 on v3

--- a/solution.py
+++ b/solution.py
@@ -158,6 +158,12 @@
     )
 
 
+STEPS = sorted(
+    ((dx, dy) for dx in range(4) for dy in range(8) if dx or dy),
+    key=lambda s: (-min(s[0], 4 - s[0]) - min(s[1], 8 - s[1]), min(s[1], 8 - s[1]), s[0], s[1]),
+)
+
+
 def wait_bytes(ref, sem):
     pltpu.make_async_copy(ref, ref, sem).wait()
 
@@ -192,8 +198,8 @@
     slot_col, fs, fr, fz, fx, fo, ts, tr, tz, tx, to, wa, wb, wl, bs, br, bz, hv, hwt, biasc,
     xs, pre, slope, ht, pp, po, gt, ta, tps, bps, tpr, bpr, fsum, fbsum, gr, gb, hg,
     s_w, r_w, s_b, r_b, s_f, r_f, s_wz, r_wz, s_bz, r_bz, s_wl, r_wl, s_wy, r_wy, s_wx, r_wx, s_fz, r_fz, s_fd, r_fd,
-    s_t, r_t, s_tz, r_tz, s_td, r_td, s_p, r_p, s_p1, r_p1, s_h, r_h, l_h, l_hw,
-    s_k, r_k, s_kb, r_kb, s_e, r_e, s_eb, r_eb,
+    s_t, r_t, s_tz, r_tz, s_td, r_td, s_h, r_h, l_h, l_hw,
+    s_k, r_k, s_kb, r_kb, s_e, r_e, s_eb, r_eb, s_p, r_p,
 ):
     zh, cc, x, zl, y = (lax.axis_index(a) for a in GRP_LRN)
     other = 1 - cc
@@ -202,9 +208,9 @@
     part = 2 * cc + zh
     own_piece = (part == x) & (x == zl)
 
-    def plane(i):
-        p = lax.rem(me + i, 32)
-        return p, lax.div(p, 8), lax.rem(p, 8)
+    def plane(step):
+        px, py = lax.rem(x + step[0], 4), lax.rem(y + step[1], 8)
+        return px * 8 + py, px, py
 
     def ring(i):
         q = lax.rem(z + i, 8)
@@ -218,8 +224,8 @@
     loads = [pltpu.make_async_copy(src, dst, in_sems.at[i]) for i, (src, dst) in enumerate(pairs)]
     barrier = pltpu.get_barrier_semaphore()
 
-    for i in range(1, 32):
-        _, px, py = plane(i)
+    for step in STEPS:
+        _, px, py = plane(step)
         pl.semaphore_signal(barrier, inc=1, device_id={"x": px, "y": py}, device_id_type=MESH)
     for i in range(1, 8):
         qh, ql = ring(i)
@@ -262,23 +268,17 @@
             remote(w.at[:, COL_DEV:], wl.at[zl], s_wl, r_wl, zh=qh, zl=ql).start()
         wl[zl] = w[:, COL_DEV:]
 
-    def go_features(i, c):
-        p, px, py = plane(i)
+    for step in STEPS:
+        p, px, py = plane(step)
         remote(fs.at[p], fr.at[me], s_f, r_f, x=px, y=py).start()
-        return c
-
-    lax.fori_loop(1, 32, go_features, 0)
     fr[me] = fs[me]
 
     @pl.when(sender)
     def _():
-        def go(i, c):
-            _, px, py = plane(i)
+        for step in STEPS:
+            _, px, py = plane(step)
             remote(w.at[:, 0:COL_DEV], wa.at[xb, zl, y], s_w, r_w, x=px, y=py).start()
             remote(bs, br.at[xb, y], s_b, r_b, x=px, y=py).start()
-            return c
-
-        lax.fori_loop(1, 32, go, 0)
         wa[xb, zl, y] = w[:, 0:COL_DEV]
         br[xb, y] = bs[...]
 
@@ -313,12 +313,9 @@
     place = jnp.where(iota((256, COL_DEV), 0) == slot_col[...], 1.0, 0.0).astype(BF)
     ts[...] = nt(place, flux[...].astype(BF)).reshape(32, 8, COL_DEV).astype(BF)
 
-    def go_targets(i, c):
-        p, px, py = plane(i)
+    for step in STEPS:
+        p, px, py = plane(step)
         remote(ts.at[p], tr.at[me], s_t, r_t, x=px, y=py).start()
-        return c
-
-    lax.fori_loop(1, 32, go_targets, 0)
     tr[me] = ts[me]
 
     @pl.when(sender)
@@ -347,7 +344,7 @@
     hw_copy.wait()
     eye = jnp.where(iota((COL_DEV, COL_DEV), 0) == iota((COL_DEV, COL_DEV), 1), 1.0, 0.0).astype(BF)
     for a in range(2):
-        hwt[a] = nt(eye, hv[a]).astype(BF)
+        hwt[a] = (0.5 * nt(eye, hv[a])).astype(BF)
     wait_bytes(tr.at[0:31], r_t)
     gott = tr[...].astype(F32).reshape(256, COL_DEV).astype(BF)
     ot = iota((64, 256), 0)
@@ -394,33 +391,31 @@
             v = v + jnp.concatenate([bc, bc], axis=1)
             sq = v * v
             t = jnp.tanh(v * (ROOT + (ROOT * CUBE) * sq))
-            cdf = 0.5 + 0.5 * t
-            ht[sb, half, r : r + 32, :] = (v * cdf).astype(BF)
+            up = 1.0 + t
+            ht[sb, half, r : r + 32, :] = (v * up).astype(BF)
             if with_slope:
-                slope[sb, r : r + 32, :] = cdf + (0.5 * v) * ((1.0 - t * t) * (ROOT + (3.0 * CUBE * ROOT) * sq))
+                slope[sb, r : r + 32, :] = up + v * ((1.0 - t * t) * (ROOT + (3.0 * CUBE * ROOT) * sq))
         return nn(hwt[half], ht[sb, half])
+
+    def swap(sb):
+        return remote(pp.at[sb], po.at[sb], s_p.at[sb], r_p.at[sb], cc=other)
 
     def forward_block(sb, c):
         pp[sb] = forward(sb, zh, True) + forward(sb, 1 - zh, False)
+        swap(sb).start()
         return c
 
     lax.fori_loop(0, 2, forward_block, 0)
-    pd = remote(pp.at[0:2], po.at[0:2], s_p, r_p, cc=other)
-    pd.start()
     fd.wait()
     gather_x(1, fo)
-    lax.fori_loop(2, 4, forward_block, 0)
-    pd1 = remote(pp.at[2:4], po.at[2:4], s_p1, r_p1, cc=other)
-    pd1.start()
-
+    lax.fori_loop(2, 3, forward_block, 0)
     wait_bytes(tx.at[0:7], r_tz)
     td = remote(tx, to, s_td, r_td, cc=other)
     td.start()
-    pd.wait()
-    pd1.wait()
-    td.wait()
+    lax.fori_loop(3, 4, forward_block, 0)
     lane0 = jnp.where(iota((8, COL_DEV), 1) == 0, 1.0, 0.0).astype(BF)
-    for sb in range(4):
+
+    def pred_grad(sb):
         src = (tx, tx, to, to)[sb]
         goal = nt(eye, src[(sb % 2) * 4 : (sb % 2) * 4 + 4].reshape(256, COL_DEV))
         flag = nt(lane0, xs[sb, :, COL_DEV:])[0:1, :]
@@ -428,31 +423,51 @@
         gt[sb] = (((pp[sb] + po[(sb + 2) % 4]) - goal) * factor).astype(BF)
 
     ones = jnp.ones((8, 256), BF)
+
+    def backward(sb, units):
+        hgrad = nn(hv[zh, units, :], gt[sb])
+        pgrad = ((0.5 * hgrad) * slope[sb, units, :]).astype(BF)
+        return nn(pgrad, xs[sb]), nt(ones, pgrad)
+
+    td.wait()
+    for sb in (2, 3):
+        swap(sb - 2).wait_recv()
+        pred_grad(sb)
+    brows = []
     for part_of in range(2):
         units = slice(part_of * 256, part_of * 256 + 256)
-        brow = jnp.zeros((8, 256), F32)
-        for sb in range(4):
-            hgrad = nn(hv[zh, units, :], gt[sb])
-            pgrad = (hgrad * slope[sb, units, :]).astype(BF)
-            term = nn(pgrad, xs[sb])
-            ta[...] = term if sb == 0 else ta[...] + term
-            brow = brow + nt(ones, pgrad)
-        tps[part_of * 16 : part_of * 16 + 16] = ta[...].reshape(16, 16, 256).astype(BF)
+        term, brow = backward(2, units)
+        ta[units, :] = term
+        term, more = backward(3, units)
+        ta[units, :] = ta[units, :] + term
+        brows.append(brow + more)
+    for sb in (0, 1):
+        swap(sb + 2).wait_recv()
+        pred_grad(sb)
+    for part_of in range(2):
+        units = slice(part_of * 256, part_of * 256 + 256)
+        brow = brows[part_of]
+        for sb in (0, 1):
+            term, more = backward(sb, units)
+            ta[units, :] = ta[units, :] + term
+            brow = brow + more
+        tps[part_of * 16 : part_of * 16 + 16] = ta[units, :].reshape(16, 16, 256).astype(BF)
         for a in range(2):
             bps[part_of * 2 + a] = brow[0:1, a * COL_DEV : (a + 1) * COL_DEV]
 
-        def go_trunk(i, c, part_of=part_of):
-            p = part_of * 16 + lax.rem(me + i, 16)
-            px, py = lax.div(p, 8), lax.rem(p, 8)
-
-            @pl.when(p != me)
-            def _():
-                remote(tps.at[p], tpr.at[me], s_k, r_k, x=px, y=py).start()
-                remote(bps.at[px], bpr.at[me], s_kb, r_kb, x=px, y=py).start()
-
-            return c
-
-        lax.fori_loop(0, 16, go_trunk, 0)
+        for dy in (4, 3, 5, 2, 6, 1, 7, 0):
+            for px in (part_of * 2, part_of * 2 + 1):
+                py = lax.rem(y + dy, 8)
+                p = px * 8 + py
+
+                def send(p=p, px=px, py=py):
+                    remote(tps.at[p], tpr.at[me], s_k, r_k, x=px, y=py).start()
+                    remote(bps.at[px], bpr.at[me], s_kb, r_kb, x=px, y=py).start()
+
+                if dy:
+                    send()
+                else:
+                    pl.when(x != px)(send)
     tpr[me] = tps[me]
     bpr[me] = bps[x]
 
@@ -460,7 +475,7 @@
         total = nt(ht[0, half], gt[0])
         for sb in range(1, 4):
             total = total + nt(ht[sb, half], gt[sb])
-        hg[half] = total
+        hg[half] = 0.5 * total
     hd = remote(hg, head.at[pl.ds(2 * cc, 2)], s_h, r_h, cc=other)
     hd.start()
     hl = pltpu.make_async_copy(hg, head.at[pl.ds(2 * cc, 2)], l_h)
@@ -505,6 +520,8 @@
 
     hl.wait()
     hd.wait_send()
+    for sb in range(4):
+        swap(sb).wait_send()
     wait_bytes(head.at[pl.ds(2 * other, 2)], r_h)
 
     @pl.when(sender)
@@ -577,10 +594,10 @@
             v((2, 4, 8, 16, c), BF), v((2, 4, 8, 16, c), BF), v((4, 16, c), BF), v((1, c), F32), v((2, 8, 1, c), F32), v((2, 4, 1, c), F32),
             v((2, 512, c), BF), v((2, c, 512), BF), v((2, 512, c), F32),
             v((4, 256, 256), BF), v((512, 256), F32), v((4, 512, 256), F32), v((4, 2, 512, 256), BF),
-            v((4, c, 256), F32), v((4, c, 256), F32), v((4, c, 256), BF), v((256, 256), F32),
+            v((4, c, 256), F32), v((4, c, 256), F32), v((4, c, 256), BF), v((512, 256), F32),
             v((32, 16, 256), BF), v((4, 1, c), F32), v((32, 16, 256), BF), v((32, 1, c), F32),
             v((16, 256), F32), v((1, c), F32), v((4, 16, 256), F32), v((4, 1, c), F32), v((2, 512, c), F32),
-        ] + [pltpu.SemaphoreType.DMA] * 42,
+        ] + [pltpu.SemaphoreType.DMA] * 38 + [pltpu.SemaphoreType.DMA((4,))] * 2,
         compiler_params=pltpu.CompilerParams(collective_id=0, has_side_effects=True),
     )(
         mass, bins, tau, mask[None], absb, alb, cosz[None], ext, ssa, asy, gas[None], sol[None], band[None],

time: 58.8 us -> 56.5 us (0.961)
  Pallas kernels: 58 us -> 55.7 us
    pallas_call x1, Pallas kernels: 55.9 us -> 53.7 us  [per_device(): pl.pallas_call(kernel, out_shape=(jax.ShapeDtypeStruct((4 * LEV, c), F32)...]
where the time goes in v4:
time: 56.5 us; the launch traced here: 56.4 us
  Pallas kernels  55.7 us (99%)
  between operations  0.65 us (1%)
    pallas_call x1, Pallas kernels, per_device(): pl.pallas_call(kernel, out_shape=(jax.ShapeDtypeStruct((4 * LEV, c), F32)...  53.7 us
    pallas_call x1, Pallas kernels, per_device(): pl.pallas_call(copy_out, out_shape=tuple((jax.ShapeDtypeStruct(a.shape, F...  2.05 us

profile of v4, /device:TPU:129, one launch (start us, length us, event | category | flops | bytes accessed | tf_op | source)
XLA Modules:
  0.0 56.4 jit_solution(11630724515541076875)
XLA Ops:
  0.6 53.7 %shard_map.192 = (f32[128,128]{1,0:T(8,128)}, f32[4,512,128]{2,1,0:T(8,128)}, f32[16,256]{1,0:T(8,128)}, f32[1,16]{1,0:T(1,128)}) custom-call(f32[4,32,128]{2,1,0:T(8,128)} %mass_in.1, s32[4,32,128]{2,1,0:T(8,128)} %bins_in.1, f32[32,128]{1,0:T(8,128)} %tau_in.1, s32[1,128]{1,0:T(1,128)} %bitcast.11, f32[32,128]{1,0:T(8,128)} %absb_in.1, f32[14,128]{1,0:T(8,128)} %alb_in.1, ...), custom_call_target="tpu_custom_call" | custom-call | tf_op jit(solution)/shard_map/pallas_call | solution.py:574
  54.3 2.1 %shard_map.193 = (f32[128,128]{1,0:T(8,128)}, f32[4,512,128]{2,1,0:T(8,128)}, f32[16,256]{1,0:T(8,128)}, f32[1,16]{1,0:T(1,128)}) custom-call(f32[128,128]{1,0:T(8,128)} %get-tuple-element.12.flux_in, f32[4,512,128]{2,1,0:T(8,128)} %get-tuple-element.13.head_in, f32[16,256]{1,0:T(8,128)} %get-tuple-element.14.tg_in, f32[1,16]{1,0:T(1,128)} %get-tuple-element.15.bg_in), custom_call_target="tpu_custom_call" | custom-call | tf_op jit(solution)/shard_map/pallas_call | solution.py:606

commit v5 on v4

--- a/solution.py
+++ b/solution.py
@@ -444,30 +444,28 @@
     for sb in (0, 1):
         swap(sb + 2).wait_recv()
         pred_grad(sb)
-    for part_of in range(2):
-        units = slice(part_of * 256, part_of * 256 + 256)
-        brow = brows[part_of]
+    for px in range(4):
+        units = slice(px * COL_DEV, px * COL_DEV + COL_DEV)
+        brow = brows[px // 2][:, (px % 2) * COL_DEV : (px % 2 + 1) * COL_DEV]
         for sb in (0, 1):
             term, more = backward(sb, units)
             ta[units, :] = ta[units, :] + term
             brow = brow + more
-        tps[part_of * 16 : part_of * 16 + 16] = ta[units, :].reshape(16, 16, 256).astype(BF)
-        for a in range(2):
-            bps[part_of * 2 + a] = brow[0:1, a * COL_DEV : (a + 1) * COL_DEV]
-
+        tps[px * 8 : px * 8 + 8] = ta[units, :].reshape(8, 16, 256).astype(BF)
+        bps[px] = brow[0:1, :]
         for dy in (4, 3, 5, 2, 6, 1, 7, 0):
-            for px in (part_of * 2, part_of * 2 + 1):
-                py = lax.rem(y + dy, 8)
-                p = px * 8 + py
-
-                def send(p=p, px=px, py=py):
-                    remote(tps.at[p], tpr.at[me], s_k, r_k, x=px, y=py).start()
-                    remote(bps.at[px], bpr.at[me], s_kb, r_kb, x=px, y=py).start()
-
-                if dy:
-                    send()
-                else:
-                    pl.when(x != px)(send)
+            py = lax.rem(y + dy, 8)
+            p = px * 8 + py
+
+            def send(p=p, px=px, py=py):
+                remote(tps.at[p], tpr.at[me], s_k, r_k, x=px, y=py).start()
+                remote(bps.at[px], bpr.at[me], s_kb, r_kb, x=px, y=py).start()
+
+            if dy:
+                send()
+            else:
+                pl.when(x != px)(send)
+
     tpr[me] = tps[me]
     bpr[me] = bps[x]
 

time: 56.5 us -> 55.7 us (0.986)
  Pallas kernels: 55.7 us -> 54.9 us
    pallas_call x1, Pallas kernels: 53.7 us -> 52.9 us  [per_device(): pl.pallas_call(kernel, out_shape=(jax.ShapeDtypeStruct((4 * LEV, c), F32)...]
where the time goes in v5:
time: 55.7 us; the launch traced here: 55.6 us
  Pallas kernels  54.9 us (99%)
  between operations  0.65 us (1%)
    pallas_call x1, Pallas kernels, per_device(): pl.pallas_call(kernel, out_shape=(jax.ShapeDtypeStruct((4 * LEV, c), F32)...  52.9 us
    pallas_call x1, Pallas kernels, per_device(): pl.pallas_call(copy_out, out_shape=tuple((jax.ShapeDtypeStruct(a.shape, F...  2.05 us

profile of v5, /device:TPU:129, one launch (start us, length us, event | category | flops | bytes accessed | tf_op | source)
XLA Modules:
  0.0 55.6 jit_solution(15095459470053267119)
XLA Ops:
  0.6 52.9 %shard_map.192 = (f32[128,128]{1,0:T(8,128)}, f32[4,512,128]{2,1,0:T(8,128)}, f32[16,256]{1,0:T(8,128)}, f32[1,16]{1,0:T(1,128)}) custom-call(f32[4,32,128]{2,1,0:T(8,128)} %mass_in.1, s32[4,32,128]{2,1,0:T(8,128)} %bins_in.1, f32[32,128]{1,0:T(8,128)} %tau_in.1, s32[1,128]{1,0:T(1,128)} %bitcast.11, f32[32,128]{1,0:T(8,128)} %absb_in.1, f32[14,128]{1,0:T(8,128)} %alb_in.1, ...), custom_call_target="tpu_custom_call" | custom-call | tf_op jit(solution)/shard_map/pallas_call | solution.py:572
  53.5 2.1 %shard_map.193 = (f32[128,128]{1,0:T(8,128)}, f32[4,512,128]{2,1,0:T(8,128)}, f32[16,256]{1,0:T(8,128)}, f32[1,16]{1,0:T(1,128)}) custom-call(f32[128,128]{1,0:T(8,128)} %get-tuple-element.12.flux_in, f32[4,512,128]{2,1,0:T(8,128)} %get-tuple-element.13.head_in, f32[16,256]{1,0:T(8,128)} %get-tuple-element.14.tg_in, f32[1,16]{1,0:T(1,128)} %get-tuple-element.15.bg_in), custom_call_target="tpu_custom_call" | custom-call | tf_op jit(solution)/shard_map/pallas_call | solution.py:604
